TPU v7x, 32 devices: a whole 2x2x4 slice. The times are simulated.
32 devices in a mesh: grp: 2 (over y), row: 16 (over z, x, core).
Axes of the slice: x: 2, y: 2, z: 4, core: 2. Of those that a mesh axis runs over, the one named last changes fastest.
Arguments:
- right_side: float32 [64, 4096], P(None, ('grp', 'row')), may hold values from -60 to 60
- links: int32 [8, 4096], P(None, ('grp', 'row')), may hold values from 0 to 4095, as said below
- coefs: float32 [4096], P(('grp', 'row')), may hold values from 0.3 to 3
- reaction: float32 [4096], P(('grp', 'row')), may hold values from 0.05 to 0.5
Outputs:
- solution: float32 [64, 4096], P(None, ('grp', 'row'))
- resid_rms: float32 [2, 64], replicated
Inputs may be any that keep to these rules, and one draw needn't show every extreme that they name: `links`: the nodes form a periodic grid of 8 x 32 x 16. Block (p, q), p < 2, q < 16, holds the nodes of first coordinate p * 4 to p * 4 + 3 and second coordinate q * 2 to q * 2 + 1, and these carry the unknowns and elements b * 4 * 2 * 16 to (b + 1) * 4 * 2 * 16 - 1, with b = p * 16 + q. Element b * 4 * 2 * 16 + (i * 2 + j) * 16 + k has its base at the node (p * 4 + i, q * 2 + j, k), and its corner l lies at the base plus (l mod 2, l // 2 mod 2, l // 4), modulo the grid. Within a block the unknowns are numbered in some order. Every unknown is a corner of 8 elements.
All inputs are finite; a program needn't handle non-finite values.
Results may differ from a plain program's by a relative error of at most 0.0003.
Values sent between devices are 32-bit elements; how exact they have to be, the bound alone decides.
A program may use at most 64 MiB of HBM per device.

v0:
```python
import functools
import math

import jax
import jax.numpy as jnp
import numpy as np
from jax import lax
from jax.experimental import pallas as pl
from jax.experimental.pallas import tpu as pltpu
from jax.sharding import PartitionSpec as P

SWEEPS = 2
DEGREE = 4
CX, CY, CZ = 4, 2, 16
SUB, LANES = 8, 128
MESH = pl.DeviceIdType.MESH
HIGHEST = lax.Precision.HIGHEST


def shifted(block, axis, distance):
    devices = range(lax.axis_size(axis))
    route = [((i - distance) % len(devices), i) for i in devices]
    return lax.ppermute(block, axis, route)


def element_matrix():
    node_ids = np.arange(8)
    corner = np.stack([node_ids % 2, node_ids // 2 % 2, node_ids // 4], axis=1)
    gauss_points = np.array([0.5 - 0.5 / math.sqrt(3.0), 0.5 + 0.5 / math.sqrt(3.0)])
    stiffness = np.zeros((8, 8))
    for q in range(8):
        quad_point = gauss_points[np.array([q % 2, q // 2 % 2, q // 4])]
        values = np.where(corner > 0.5, quad_point, 1.0 - quad_point)
        slopes = np.where(corner > 0.5, 1.0, -1.0)
        gradient = np.stack(
            [
                slopes[:, 0] * values[:, 1] * values[:, 2],
                values[:, 0] * slopes[:, 1] * values[:, 2],
                values[:, 0] * values[:, 1] * slopes[:, 2],
            ],
            axis=1,
        )
        stiffness = stiffness + gradient @ gradient.T / 8.0
    return stiffness


def element_images(window, offsets, weights, stiffness):
    corners = window[:, offsets]
    images = (
        jnp.einsum("ml,rle->rme", stiffness, corners, precision=lax.Precision.HIGHEST) * weights
    )
    return jnp.zeros_like(window).at[:, offsets].add(images)


def on_device(right_side, links, coefs, reaction):
    stiffness = jnp.asarray(element_matrix(), dtype=jnp.float32)
    count = right_side.shape[1]
    groups = lax.axis_size("grp")
    rowcount = lax.axis_size("row")
    group_id = lax.axis_index("grp")
    row_id = lax.axis_index("row")
    total = count * groups * rowcount
    owner = links // count
    slot = links % count
    first = jnp.mod(owner // rowcount - group_id, groups)
    second = jnp.mod(owner % rowcount - row_id, rowcount)
    offsets = (first * 2 + second) * count + slot

    def apply_operator(field):
        above_row = shifted(field, "row", -1)
        upper = shifted(jnp.stack([field, above_row], axis=0), "grp", -1)
        window = jnp.concatenate([field, above_row, upper[0], upper[1]], axis=1)
        summed = element_images(window, offsets, coefs, stiffness)
        back = shifted(
            jnp.stack([summed[:, 2 * count : 3 * count], summed[:, 3 * count :]], axis=0), "grp", 1
        )
        first_col = summed[:, :count] + back[0]
        second_col = summed[:, count : 2 * count] + back[1]
        first_col = first_col + shifted(second_col, "row", 1)
        return first_col + reaction * field

    image = apply_operator(right_side)
    cross, square = lax.psum(
        (jnp.sum(right_side * image, axis=1), jnp.sum(image * image, axis=1)), ("grp", "row")
    )
    theta = square / cross
    upper = (1.5 * theta)[:, None]
    lower = upper / 10.0
    center = (upper + lower) / 2.0
    half = (upper - lower) / 2.0
    sigma = center / half
    solution = jnp.zeros_like(right_side)
    residual = right_side
    history = []
    for sweep in range(SWEEPS):
        start = residual
        correction = jnp.zeros_like(right_side)
        rho_now = 1.0 / sigma
        direction = residual / center
        for step in range(DEGREE):
            correction = correction + direction
            residual = residual - apply_operator(direction)
            if step + 1 < DEGREE:
                rho_next = 1.0 / (2.0 * sigma - rho_now)
                direction = rho_next * rho_now * direction + 2.0 * rho_next / half * residual
                rho_now = rho_next
        change = start - residual
        along, length, begin = lax.psum(
            (
                jnp.sum(start * change, axis=1),
                jnp.sum(change * change, axis=1),
                jnp.sum(start * start, axis=1),
            ),
            ("grp", "row"),
        )
        omega = along / length
        residual = start - omega[:, None] * change
        squares = begin - 2.0 * omega * along + omega * omega * length
        solution = solution + omega[:, None] * correction
        history.append(jnp.sqrt(squares / total))
    return (solution, jnp.stack(history, axis=0))


def next_x(plane):
    return jnp.concatenate([plane[1:], plane[:1]], axis=0)


def last_x(plane):
    return jnp.concatenate([plane[-1:], plane[:-1]], axis=0)


def next_z(plane):
    turned = pltpu.roll(plane, SUB - 1, 1)
    place = lax.broadcasted_iota(jnp.int32, plane.shape, 1)
    return jnp.where(place == SUB - 1, pltpu.roll(turned, LANES // 2, 2), turned)


def last_z(plane):
    turned = pltpu.roll(plane, 1, 1)
    place = lax.broadcasted_iota(jnp.int32, plane.shape, 1)
    return jnp.where(place == 0, pltpu.roll(turned, LANES // 2, 2), turned)


def two_sum(a, b):
    total = a + b
    part = total - a
    return total, (a - (total - part)) + (b - part)


def halves(a):
    scaled = 4097.0 * a
    high = scaled - (scaled - a)
    return high, a - high


def scaled_sum(weights, pairs):
    total = rest = None
    for weight, (value, error) in zip(weights, pairs):
        product = weight * value
        weight_high, weight_low = halves(weight)
        high, low = halves(value)
        lost = ((weight_high * high - product) + weight_high * low + weight_low * high) + weight_low * low
        lost = lost + weight * error
        if total is None:
            total, rest = product, lost
        else:
            total, error = two_sum(total, product)
            rest = rest + (error + lost)
    return total, rest


def chebyshev_weights(theta):
    upper = 1.5 * theta
    lower = upper / 10.0
    center = (upper + lower) / 2.0
    half = (upper - lower) / 2.0
    sigma = center / half
    rho_now = 1.0 / sigma
    direction = [1.0 / center]
    residual = [jnp.ones_like(theta)]
    correction = []
    for step in range(DEGREE):
        size = len(direction)
        correction = [
            direction[k] + correction[k] if k < len(correction) else direction[k]
            for k in range(size)
        ]
        residual = [residual[0]] + [
            residual[k] - direction[k - 1] if k < len(residual) else -direction[k - 1]
            for k in range(1, size + 1)
        ]
        if step + 1 < DEGREE:
            rho_next = 1.0 / (2.0 * sigma - rho_now)
            direction = [
                rho_next * rho_now * direction[k] + 2.0 * rho_next / half * residual[k]
                if k < size
                else 2.0 * rho_next / half * residual[k]
                for k in range(size + 1)
            ]
            rho_now = rho_next
    return correction, [-value for value in residual[1:]]


def kernel(
    groups, rowcount, total,
    right_ref, links_ref, coefs_ref, react_ref,
    packed_ref,
    field, mass, diag, edge_x, edge_y, edge_z, aux,
    power1, power2, power3, power4, grams, sums,
    field_send, field_recv, aux_send, aux_recv, sums_send, sums_recv,
):
    half_reach = DEGREE // CY
    reach = SWEEPS * half_reach
    grp = lax.axis_index("grp")
    row = lax.axis_index("row")
    own = range(reach * CY, reach * CY + CY)
    nrhs = right_ref.shape[0]
    count = right_ref.shape[1]

    def row_at(offset):
        return lax.rem(row + offset + rowcount, rowcount)

    far = sorted(range(-reach, reach + 1), key=lambda o: (abs(o) > half_reach, -abs(o)))
    near = [(o, d) for o in far for d in range(groups)]
    near = [(o, d) for o, d in near if o or d]

    barrier = pltpu.get_barrier_semaphore()
    greeted = 0
    for o in range(1, rowcount):
        pl.semaphore_signal(barrier, inc=1, device_id=(grp, row_at(o)), device_id_type=MESH)
        greeted += 1
    for o, d in near:
        if d:
            peer = (lax.rem(grp + d, groups), row_at(o))
            pl.semaphore_signal(barrier, inc=1, device_id=peer, device_id_type=MESH)
            greeted += 1

    home = (grp * rowcount + row) * count
    slots = jnp.broadcast_to(links_ref[0:1, :] - home, (count, count))
    slot_of = (slots == lax.broadcasted_iota(jnp.int32, (count, count), 0)).astype(jnp.float32)
    order = jnp.transpose(slot_of)
    lanes = lax.broadcasted_iota(jnp.int32, (CX, SUB, LANES), 2)
    low = lanes < LANES // 2
    react = jnp.dot(
        jnp.broadcast_to(react_ref[...], (SUB, count)), slot_of,
        precision=HIGHEST, preferred_element_type=jnp.float32,
    )
    which = lax.broadcasted_iota(jnp.int32, (SUB, count), 0)
    my_aux = reach * groups + grp
    aux[my_aux] = jnp.where(
        which == 0, jnp.broadcast_to(coefs_ref[...], (SUB, count)) * (1.0 / 12.0), react
    )
    twice = jnp.concatenate([right_ref[...], right_ref[...]], axis=0)
    nodes = lax.dot_general(
        order, twice, (((1,), (1,)), ((), ())), precision=HIGHEST,
        preferred_element_type=jnp.float32,
    ).reshape(CX, CY, 2, SUB, LANES)
    for y in range(CY):
        field[reach * CY + y, pl.ds(grp * CX, CX)] = jnp.where(low, nodes[:, y, 0], nodes[:, y, 1])

    pl.semaphore_wait(barrier, greeted)
    aux_copies, field_copies = [], []
    for k, (o, d) in enumerate(near):
        peer = (lax.rem(grp + d, groups), row_at(o))
        copy = pltpu.make_async_remote_copy(
            src_ref=aux.at[my_aux], dst_ref=aux.at[(reach - o) * groups + grp],
            send_sem=aux_send.at[k], recv_sem=aux_recv.at[k], device_id=peer, device_id_type=MESH,
        )
        copy.start()
        aux_copies.append(copy)
    for k, (o, d) in enumerate(near):
        peer = (lax.rem(grp + d, groups), row_at(o))
        copy = pltpu.make_async_remote_copy(
            src_ref=field.at[pl.ds(reach * CY, CY), pl.ds(grp * CX, CX)],
            dst_ref=field.at[pl.ds((reach - o) * CY, CY), pl.ds(grp * CX, CX)],
            send_sem=field_send.at[k], recv_sem=field_recv.at[k], device_id=peer, device_id_type=MESH,
        )
        copy.start()
        field_copies.append(copy)

    blocks = 2 * reach + 1
    planes = blocks * CY
    inner = [abs(o) <= half_reach for o, d in near]
    low_plane, top_plane = half_reach * CY, planes - half_reach * CY

    def expand(begin, end):
        table = aux[begin * groups : end * groups].reshape((end - begin) * groups * SUB, count)
        spare = -table.shape[0] % count
        table = jnp.concatenate([table, jnp.zeros((spare, count), jnp.float32)], axis=0)
        columns = [
            jnp.transpose(table[k : k + count]).reshape(CX, CY, 2, SUB, LANES)
            for k in range(0, table.shape[0], count)
        ]
        for b in range(begin, end):
            for g in range(groups):
                for y in range(CY):
                    for entry, target in ((0, mass), (1, diag)):
                        part, at = divmod(((b - begin) * groups + g) * SUB + entry, count)
                        part = columns[part]
                        first = jnp.broadcast_to(part[:, y, 0, :, at : at + 1], (CX, SUB, LANES))
                        second = jnp.broadcast_to(part[:, y, 1, :, at : at + 1], (CX, SUB, LANES))
                        target[b * CY + y, g * CX : (g + 1) * CX] = jnp.where(low, first, second)

    def edges(begin, end):
        before_xz = before_x = before_z = None
        for y in range(begin, end):
            here = mass[y]
            here_z = here + last_z(here)
            here_x = here + last_x(here)
            here_xz = here_z + last_x(here_z)
            edge_y[y] = here_xz
            if y > begin:
                edge_x[y] = here_z + before_z
                edge_z[y] = here_x + before_x
                diag[y] = diag[y] + 5.0 * (here_xz + before_xz)
            before_xz, before_x, before_z = here_xz, here_x, here_z

    for copy, is_inner in zip(aux_copies, inner):
        if is_inner:
            copy.wait_recv()
    expand(half_reach, blocks - half_reach)
    edges(low_plane, top_plane - 1)

    def apply_operator(source, target, begin, end):
        def gathered(y):
            value = source[y]
            above = next_z(value)
            pair = value + above
            return value, above, pair + next_x(pair)

        last, _, last_sum = gathered(begin - 1)
        value, above, here_sum = gathered(begin)
        last_push = mass[begin - 1] * (last_sum + here_sum)
        for y in range(begin, end):
            following, following_above, following_sum = gathered(y + 1)
            push = mass[y] * (here_sum + following_sum)
            push_y = push + last_push
            push_x = push_y + last_x(push_y)
            result = diag[y] * value - push_x + edge_z[y] * above
            result = result + edge_x[y] * next_x(value) + last_x(edge_x[y] * value)
            result = result + edge_y[y] * following + edge_y[y - 1] * last
            target[y] = result + last_z(edge_z[y] * value - push_x)
            last, last_push = value, push
            value, above, here_sum = following, following_above, following_sum

    def across(products):
        return jnp.sum(jnp.sum(products, axis=0), axis=0, keepdims=True)

    def start_sum(number, slots, rows):
        rows = rows + [jnp.zeros_like(rows[0])] * (slots.shape[1] - len(rows))
        slots[row] = jnp.concatenate(rows, axis=0)
        copies = []
        for o in sorted(range(1, rowcount), key=lambda o: -min(o, rowcount - o)):
            copy = pltpu.make_async_remote_copy(
                src_ref=slots.at[row], dst_ref=slots.at[row],
                send_sem=sums_send.at[number, o - 1], recv_sem=sums_recv.at[number, o - 1],
                device_id=(grp, row_at(o)), device_id_type=MESH,
            )
            copy.start()
            copies.append(copy)
        return copies

    def end_sum(slots, copies):
        for copy in copies:
            copy.wait_recv()
        added, rest = slots[0], jnp.zeros_like(slots[0])
        for k in range(1, rowcount):
            added, error = two_sum(added, slots[k])
            rest = rest + error
        added, error = two_sum(added, pltpu.roll(added, LANES // 2, 1))
        return added, rest + pltpu.roll(rest, LANES // 2, 1) + error

    def spread(line):
        return jnp.broadcast_to(line, (SUB, LANES))

    def combined(weights, powers, y):
        value = weights[0] * powers[0][y]
        for weight, power in zip(weights[1:], powers[1:]):
            value = value + weight * power[y]
        return value

    for copy, is_inner in zip(field_copies, inner):
        if is_inner:
            copy.wait_recv()
    powers = [field, power1, power2, power3, power4]
    for k in range(DEGREE):
        apply_operator(powers[k], powers[k + 1], low_plane + k + 1, top_plane - k - 1)
    pairs = [(j, k) for j in range(DEGREE + 1) for k in range(max(j, 1), DEGREE + 1)]
    products = [
        across(sum(powers[j][y] * powers[k][y] for y in own)) for j, k in pairs
    ]
    bound = start_sum(0, grams, products)
    for copy, is_inner in zip(aux_copies, inner):
        if not is_inner:
            copy.wait_recv()
    expand(0, half_reach)
    expand(blocks - half_reach, blocks)
    edges(0, low_plane + 1)
    edges(top_plane - 2, planes - 1)
    for copy, is_inner in zip(field_copies, inner):
        if not is_inner:
            copy.wait_recv()
    for k in range(DEGREE):
        apply_operator(powers[k], powers[k + 1], k + 1, low_plane + k + 1)
        apply_operator(powers[k], powers[k + 1], top_plane - k - 1, planes - k - 1)

    half_rows = [order.reshape(CX, CY, 2, SUB, count)[:, :, z] for z in range(2)]
    half_rows = [
        jnp.concatenate([part[:, y].reshape(CX * SUB, count) for y in range(CY)], axis=0)
        for part in half_rows
    ]

    def mine(y, value):
        return jnp.where(grp == 0, value[:CX], value[CX:])

    def to_slots(parts):
        stacked = jnp.concatenate([part.reshape(CX * SUB, LANES) for part in parts], axis=0)
        turned = jnp.transpose(stacked)
        return sum(
            jnp.dot(
                turned[z * nrhs : (z + 1) * nrhs], half_rows[z],
                precision=HIGHEST, preferred_element_type=jnp.float32,
            )
            for z in range(2)
        )

    added, rest = end_sum(grams, bound)
    gram = {
        pair: (spread(added[at : at + 1]), spread(rest[at : at + 1])) for at, pair in enumerate(pairs)
    }
    correct, differ = chebyshev_weights(gram[1, 1][0] / gram[0, 1][0])
    along = scaled_sum(differ, [gram[0, k] for k in range(1, DEGREE + 1)])
    length = scaled_sum(
        differ,
        [
            scaled_sum(differ, [gram[min(j, k), max(j, k)] for k in range(1, DEGREE + 1)])
            for j in range(1, DEGREE + 1)
        ],
    )
    omega = (along[0] + along[1]) / (length[0] + length[1])
    corrections = [omega * mine(y, combined(correct, powers[:-1], y)) for y in own]
    for copy in field_copies:
        copy.wait_send()
    steps = [omega * weight for weight in differ]
    for y in range(low_plane, top_plane):
        field[y] = field[y] - combined(steps, powers[1:], y)
    for k in range(DEGREE):
        apply_operator(powers[k], powers[k + 1], low_plane + k + 1, top_plane - k - 1)
    along = length = begin = 0.0
    for y in own:
        change = combined(differ, powers[1:], y)
        along = along + across(field[y] * change)
        length = length + across(change * change)
        begin = begin + across(field[y] * field[y])
    step_sum = start_sum(1, sums, [along, length, begin])
    settled = to_slots(corrections)
    later = to_slots([mine(y, combined(correct, powers[:-1], y)) for y in own])
    added = sum(end_sum(sums, step_sum))
    along, length, begin = (spread(added[k : k + 1]) for k in range(3))
    omega = along / length
    first_rms = jnp.sqrt(begin / total)
    second_rms = jnp.sqrt((begin - 2.0 * omega * along + omega * omega * length) / total)
    packed_ref[pl.ds(nrhs, SUB)] = jnp.where(
        lax.broadcasted_iota(jnp.int32, (SUB, LANES), 0) == 0, first_rms, second_rms
    )
    column = jnp.transpose(jnp.broadcast_to(omega[0:1], (LANES, LANES)))[:nrhs]
    packed_ref[pl.ds(0, nrhs)] = settled + column * later
    for copy in aux_copies + bound + step_sum:
        copy.wait_send()


def unpack(packed_ref, out_ref, rms_ref):
    nrhs = out_ref.shape[0]
    out_ref[...] = packed_ref[:nrhs]
    rms_ref[...] = packed_ref[nrhs : nrhs + SWEEPS, :nrhs]


def whole_sweeps(groups, rowcount, right_side, links, coefs, reaction):
    nrhs, count = right_side.shape
    reach = SWEEPS * (DEGREE // CY)
    planes = (2 * reach + 1) * CY
    window = pltpu.VMEM((planes, groups * CX, SUB, LANES), jnp.float32)
    nears = groups * (2 * reach + 1) - 1
    dma = pltpu.SemaphoreType.DMA
    vmem = pl.BlockSpec(memory_space=pltpu.VMEM)
    packed = pl.pallas_call(
        functools.partial(kernel, groups, rowcount, count * groups * rowcount),
        out_shape=jax.ShapeDtypeStruct((nrhs + SUB, count), jnp.float32),
        in_specs=[vmem] * 4,
        out_specs=vmem,
        scratch_shapes=[
            window, window, window, window, window, window,
            pltpu.VMEM(((2 * reach + 1) * groups, SUB, count), jnp.float32),
            window, window, window, window,
            pltpu.VMEM((rowcount, 2 * SUB, LANES), jnp.float32),
            pltpu.VMEM((rowcount, 4, LANES), jnp.float32),
            dma((nears,)), dma((nears,)), dma((nears,)), dma((nears,)),
            dma((SWEEPS, rowcount - 1)), dma((SWEEPS, rowcount - 1)),
        ],
        compiler_params=pltpu.CompilerParams(collective_id=0, has_side_effects=True),
    )(right_side, links, coefs.reshape(1, count), reaction.reshape(1, count))
    return pl.pallas_call(
        unpack,
        out_shape=(
            jax.ShapeDtypeStruct((nrhs, count), jnp.float32),
            jax.ShapeDtypeStruct((SWEEPS, nrhs), jnp.float32),
        ),
        in_specs=[vmem],
        out_specs=(vmem, vmem),
    )(packed)


def in_one_kernel(mesh):
    return mesh.shape["grp"] == 2 and mesh.shape["row"] >= 2 * SWEEPS * (DEGREE // CY) + 1


def solution(mesh):
    body = on_device
    if in_one_kernel(mesh):
        body = functools.partial(whole_sweeps, mesh.shape["grp"], mesh.shape["row"])
    return jax.shard_map(
        body,
        mesh=mesh,
        in_specs=(
            P(None, ("grp", "row")),
            P(None, ("grp", "row")),
            P(("grp", "row")),
            P(("grp", "row")),
        ),
        out_specs=(P(None, ("grp", "row")), P()),
        check_vma=False,
    )
```

profile of v0, /device:TPU:0, one launch (start us, length us, event | category | flops | bytes accessed | tf_op | source)
XLA Modules:
  0.0 30.7 jit_solution(11320453053888866261)
XLA Ops:
  0.6 28.6 %shard_map.59.packed_ref = f32[72,128]{1,0:T(8,128)} custom-call(f32[64,128]{1,0:T(8,128)} %right_ref.1, s32[8,128]{1,0:T(8,128)} %links_ref.1, f32[1,128]{1,0:T(1,128)} %bitcast.2, f32[1,128]{1,0:T(1,128)} %bitcast.3), custom_call_target="tpu_custom_call" | custom-call | tf_op jit(solution)/shard_map/pallas_call | solution.py:486
  29.3 1.4 %shard_map.60 = (f32[64,128]{1,0:T(8,128)}, f32[2,64]{1,0:T(2,128)}) custom-call(f32[72,128]{1,0:T(8,128)} %shard_map.59.packed_ref), custom_call_target="tpu_custom_call" | custom-call | tf_op jit(solution)/shard_map/pallas_call | solution.py:502
where the time goes:
time: 30.9 us; the launch traced here: 30.7 us
  Pallas kernels  30 us (97%)
  between operations  0.64 us (2%)
    pallas_call x1, Pallas kernels, whole_sweeps(): pl.pallas_call(functools.partial(kernel, groups, rowcount, count * groups...  28.6 us
    pallas_call x1, Pallas kernels, whole_sweeps(): pl.pallas_call(unpack, out_shape=(jax.ShapeDtypeStruct((nrhs, count), jnp...  1.39 us

commit v1 on v0

v1 whole, which is shorter than its diff:
```python
import functools
import math

import jax
import jax.numpy as jnp
import numpy as np
from jax import lax
from jax.experimental import pallas as pl
from jax.experimental.pallas import tpu as pltpu
from jax.sharding import PartitionSpec as P

SWEEPS = 2
DEGREE = 4
CX, CY, CZ = 4, 2, 16
SUB, LANES = 8, 128
MESH = pl.DeviceIdType.MESH
HIGHEST = lax.Precision.HIGHEST


def shifted(block, axis, distance):
    devices = range(lax.axis_size(axis))
    route = [((i - distance) % len(devices), i) for i in devices]
    return lax.ppermute(block, axis, route)


def element_matrix():
    node_ids = np.arange(8)
    corner = np.stack([node_ids % 2, node_ids // 2 % 2, node_ids // 4], axis=1)
    gauss_points = np.array([0.5 - 0.5 / math.sqrt(3.0), 0.5 + 0.5 / math.sqrt(3.0)])
    stiffness = np.zeros((8, 8))
    for q in range(8):
        quad_point = gauss_points[np.array([q % 2, q // 2 % 2, q // 4])]
        values = np.where(corner > 0.5, quad_point, 1.0 - quad_point)
        slopes = np.where(corner > 0.5, 1.0, -1.0)
        gradient = np.stack(
            [
                slopes[:, 0] * values[:, 1] * values[:, 2],
                values[:, 0] * slopes[:, 1] * values[:, 2],
                values[:, 0] * values[:, 1] * slopes[:, 2],
            ],
            axis=1,
        )
        stiffness = stiffness + gradient @ gradient.T / 8.0
    return stiffness


def element_images(window, offsets, weights, stiffness):
    corners = window[:, offsets]
    images = (
        jnp.einsum("ml,rle->rme", stiffness, corners, precision=lax.Precision.HIGHEST) * weights
    )
    return jnp.zeros_like(window).at[:, offsets].add(images)


def on_device(right_side, links, coefs, reaction):
    stiffness = jnp.asarray(element_matrix(), dtype=jnp.float32)
    count = right_side.shape[1]
    groups = lax.axis_size("grp")
    rowcount = lax.axis_size("row")
    group_id = lax.axis_index("grp")
    row_id = lax.axis_index("row")
    total = count * groups * rowcount
    owner = links // count
    slot = links % count
    first = jnp.mod(owner // rowcount - group_id, groups)
    second = jnp.mod(owner % rowcount - row_id, rowcount)
    offsets = (first * 2 + second) * count + slot

    def apply_operator(field):
        above_row = shifted(field, "row", -1)
        upper = shifted(jnp.stack([field, above_row], axis=0), "grp", -1)
        window = jnp.concatenate([field, above_row, upper[0], upper[1]], axis=1)
        summed = element_images(window, offsets, coefs, stiffness)
        back = shifted(
            jnp.stack([summed[:, 2 * count : 3 * count], summed[:, 3 * count :]], axis=0), "grp", 1
        )
        first_col = summed[:, :count] + back[0]
        second_col = summed[:, count : 2 * count] + back[1]
        first_col = first_col + shifted(second_col, "row", 1)
        return first_col + reaction * field

    image = apply_operator(right_side)
    cross, square = lax.psum(
        (jnp.sum(right_side * image, axis=1), jnp.sum(image * image, axis=1)), ("grp", "row")
    )
    theta = square / cross
    upper = (1.5 * theta)[:, None]
    lower = upper / 10.0
    center = (upper + lower) / 2.0
    half = (upper - lower) / 2.0
    sigma = center / half
    solution = jnp.zeros_like(right_side)
    residual = right_side
    history = []
    for sweep in range(SWEEPS):
        start = residual
        correction = jnp.zeros_like(right_side)
        rho_now = 1.0 / sigma
        direction = residual / center
        for step in range(DEGREE):
            correction = correction + direction
            residual = residual - apply_operator(direction)
            if step + 1 < DEGREE:
                rho_next = 1.0 / (2.0 * sigma - rho_now)
                direction = rho_next * rho_now * direction + 2.0 * rho_next / half * residual
                rho_now = rho_next
        change = start - residual
        along, length, begin = lax.psum(
            (
                jnp.sum(start * change, axis=1),
                jnp.sum(change * change, axis=1),
                jnp.sum(start * start, axis=1),
            ),
            ("grp", "row"),
        )
        omega = along / length
        residual = start - omega[:, None] * change
        squares = begin - 2.0 * omega * along + omega * omega * length
        solution = solution + omega[:, None] * correction
        history.append(jnp.sqrt(squares / total))
    return (solution, jnp.stack(history, axis=0))


def thirds(a):
    high = a.astype(jnp.bfloat16).astype(jnp.float32)
    rest = a - high
    middle = rest.astype(jnp.bfloat16).astype(jnp.float32)
    return [high, middle, rest - middle]


def added(parts):
    high, middle, low = parts
    return high + middle + low


def turned(a, distance, axis=1):
    return pltpu.roll(a, distance % a.shape[axis], axis)


def chebyshev_steps():
    sigma = (1.5 + 0.15) / (1.5 - 0.15)
    rho_now = 1.0 / sigma
    steps = []
    for _ in range(DEGREE - 1):
        rho_next = 1.0 / (2.0 * sigma - rho_now)
        steps.append((rho_next * rho_now, 2.0 * rho_next / ((1.5 - 0.15) / 2.0)))
        rho_now = rho_next
    return 2.0 / (1.5 + 0.15), steps


def kernel(
    groups, rowcount, total,
    right_ref, links_ref, coefs_ref, react_ref,
    packed_ref,
    outbox, inbox, answers, solved, weights, order,
    bases, changes, directions, corrections, residuals, settled,
    out_send, out_recv, back_send, back_recv,
):
    nrhs, count = right_ref.shape
    leaders = nrhs // SUB
    heads = leaders // groups
    blocks = groups * rowcount
    half_lane = CX
    z_lane = CX * CY
    grp = lax.axis_index("grp")
    row = lax.axis_index("row")
    me = grp * rowcount + row
    leading = row < heads
    rank = grp * heads + row

    def leader(t):
        return (t // heads, lax.rem(t, heads))

    def block(b):
        return (b // rowcount, lax.rem(b, rowcount))

    def place_of(t):
        return (t // heads) * rowcount + lax.rem(t, heads)

    barrier = pltpu.get_barrier_semaphore()

    @pl.when(leading)
    def _():
        for o in range(1, blocks):
            pl.semaphore_signal(
                barrier, inc=1, device_id=block(lax.rem(me + o, blocks)), device_id_type=MESH
            )

    lane = lax.broadcasted_iota(jnp.int32, (count, count), 1)
    down = lax.broadcasted_iota(jnp.int32, (count, count), 0)
    element = ((lane % CX) * CY + lane // CX % CY) * CZ + lane // z_lane
    to_lanes = (down == element).astype(jnp.float32)
    slots = (links_ref[0:1, :] - me * count).astype(jnp.float32)
    mass = thirds(coefs_ref[...] * (1.0 / 12.0))
    small = jnp.concatenate([slots] + mass + [jnp.zeros((SUB - 4, count), jnp.float32)], axis=0)
    small = jnp.dot(small, to_lanes, preferred_element_type=jnp.float32)
    mass = added([small[k : k + 1] for k in (1, 2, 3)])
    order[...] = (down.astype(jnp.float32) == small[0:1]).astype(jnp.float32)
    react = thirds(react_ref[...])
    react = jnp.concatenate(react + [jnp.zeros((SUB - 3, count), jnp.float32)], axis=0)
    stack = jnp.concatenate(thirds(right_ref[...]) + [react], axis=0)
    stack = jnp.dot(stack, order[...], preferred_element_type=jnp.float32)
    field = added([stack[k * nrhs : (k + 1) * nrhs] for k in range(3)])
    react = added([stack[3 * nrhs + k : 3 * nrhs + k + 1] for k in range(3)])
    extra = jnp.concatenate([mass, react], axis=0)
    for t in range(leaders):
        outbox[t, 0:SUB] = field[t * SUB : (t + 1) * SUB]
        outbox[t, SUB : SUB + 2] = extra

    pl.semaphore_wait(barrier, jnp.where(leading, leaders - 1, leaders))

    def post(o):
        t = lax.rem(rank + o, leaders)
        return pltpu.make_async_remote_copy(
            src_ref=outbox.at[t], dst_ref=inbox.at[me],
            send_sem=out_send.at[t], recv_sem=out_recv.at[me],
            device_id=leader(t), device_id_type=MESH,
        )

    for o in range(1, leaders):
        post(o).start()

    @pl.when(jnp.logical_not(leading))
    def _():
        post(0).start()

    def reply(b):
        return pltpu.make_async_remote_copy(
            src_ref=solved.at[b], dst_ref=answers.at[rank],
            send_sem=back_send.at[b], recv_sem=back_recv.at[rank],
            device_id=block(b), device_id_type=MESH,
        )

    @pl.when(leading)
    def _():
        inbox[me] = outbox[rank]
        for o in range(1, blocks):
            b = lax.rem(me + o, blocks)
            pltpu.make_async_remote_copy(
                src_ref=outbox.at[0], dst_ref=inbox.at[b],
                send_sem=out_send.at[0], recv_sem=out_recv.at[b],
                device_id=block(b), device_id_type=MESH,
            ).wait_recv()

        rows_lane = lax.broadcasted_iota(jnp.int32, (rowcount, count), 1)
        in_second = rows_lane // CX % CY == 1
        in_first = rows_lane % CX > 0
        plus, minus = [], []
        for p in range(groups):
            m = inbox[p * rowcount : (p + 1) * rowcount, SUB, :]
            up4, up12 = turned(m, half_lane), turned(m, half_lane + z_lane)
            down4 = turned(m, -half_lane)
            plus.append([
                m,
                turned(m, z_lane),
                jnp.where(in_second, up4, turned(down4, 1, 0)),
                jnp.where(in_second, up12, turned(up4, 1, 0)),
            ])
        for p in range(groups):
            before = plus[(p - 1) % groups]
            minus.append([
                jnp.where(in_first, turned(m, 1), turned(other, 1 - CX))
                for m, other in zip(plus[p], before)
            ])
        for p in range(groups):
            rows = slice(p * rowcount, (p + 1) * rowcount)
            both = [-(a + b) for a, b in zip(plus[p], minus[p])]
            diag = inbox[rows, SUB + 1, :] - 4.0 * (both[0] + both[1] + both[2] + both[3])
            for k in range(4):
                weights[k, rows] = -minus[p][k]
                weights[4 + k, rows] = -plus[p][k]
                weights[8 + k, rows] = both[k]
            weights[12, rows] = diag

        tile_lane = lax.broadcasted_iota(jnp.int32, (SUB, count), 1)
        is_second = tile_lane // CX % CY == 1
        first_low = tile_lane % CX == 0
        first_top = tile_lane % CX == CX - 1

        def apply_operator(source, sink):
            rolled = {}

            def rolls(p, q):
                q = q % rowcount
                if (p, q) not in rolled:
                    v = source(p * rowcount + q)
                    near = half_lane
                    rolled[p, q] = (
                        v, turned(v, -z_lane), turned(v, z_lane),
                        turned(v, near), turned(v, -near),
                        turned(v, near + z_lane), turned(v, -near - z_lane),
                    )
                return rolled[p, q]

            for q in range(rowcount):
                forward, backward, middle = [], [], []
                for p in range(groups):
                    b = p * rowcount + q
                    v, above, below, up4, down4, up12, down12 = rolls(p, q)
                    _, _, _, next4, nextd4, next12, _ = rolls(p, q + 1)
                    _, _, _, last4, lastd4, _, lastd12 = rolls(p, q - 1)
                    near = jnp.where(is_second, next4, down4)
                    far = jnp.where(is_second, up4, lastd4)
                    diagonal = [
                        jnp.where(is_second, nextd4, down12),
                        jnp.where(is_second, next12, up4),
                        jnp.where(is_second, down4, lastd12),
                        jnp.where(is_second, up12, last4),
                    ]
                    sides = [
                        above + (near + diagonal[0]),
                        below + (near + diagonal[1]),
                        above + (far + diagonal[2]),
                        below + (far + diagonal[3]),
                    ]
                    w = [weights[k, b : b + 1, :] for k in range(13)]
                    forward.append(
                        (w[0] * sides[0] + w[1] * sides[1]) + (w[2] * sides[2] + w[3] * sides[3])
                    )
                    backward.append(
                        (w[4] * sides[0] + w[5] * sides[1]) + (w[6] * sides[2] + w[7] * sides[3])
                    )
                    middle.append(
                        (w[8] * diagonal[0] + w[9] * diagonal[1])
                        + (w[10] * diagonal[2] + w[11] * diagonal[3])
                        + w[12] * v
                    )
                for p in range(groups):
                    after, before = (p + 1) % groups, (p - 1) % groups
                    ahead = jnp.where(first_top, turned(forward[after], CX - 1), turned(forward[p], -1))
                    behind = jnp.where(
                        first_low, turned(backward[before], 1 - CX), turned(backward[p], 1)
                    )
                    sink(p * rowcount + q, middle[p] + (ahead + behind))

        def across(parts):
            total_ = (parts[0] + parts[1]) + (parts[2] + parts[3])
            return jnp.broadcast_to(jnp.sum(total_, axis=1, keepdims=True), (SUB, count))

        class Sum:
            def __init__(self):
                self.parts = [None] * 4
                self.at = 0

            def add(self, value):
                k = self.at % 4
                self.parts[k] = value if self.parts[k] is None else self.parts[k] + value
                self.at += 1

            def get(self):
                return across(self.parts)

        scale, steps = chebyshev_steps()
        square, cross = Sum(), Sum()

        def first_image(b, image):
            start = inbox[b, 0:SUB]
            residuals[b] = image
            square.add(image * image)
            cross.add(start * image)

        apply_operator(lambda b: inbox[b, 0:SUB], first_image)
        inverse = cross.get() / square.get()
        opening = scale * inverse

        first_rms = second_rms = None
        omegas = []
        for sweep in range(SWEEPS):
            along, length, begin = Sum(), Sum(), Sum()
            start_of = (lambda b: inbox[b, 0:SUB]) if sweep == 0 else (lambda b: bases[b])
            for step in range(DEGREE):
                here, there = directions.at[step % 2], directions.at[(step + 1) % 2]

                def finish(b, image, step=step, here=here, there=there, sweep=sweep):
                    before = start_of(b) if step == 0 else residuals[b]
                    direction = here[b]
                    residual = before - image
                    if step + 1 < DEGREE:
                        keep, gain = steps[step]
                        following = keep * direction + (gain * inverse) * residual
                        residuals[b] = residual
                        there[b] = following
                        so_far = direction if step == 0 else corrections[sweep, b]
                        corrections[sweep, b] = so_far + following
                    else:
                        start = start_of(b)
                        change = start - residual
                        changes[b] = change
                        along.add(start * change)
                        length.add(change * change)

                if sweep == 0 and step == 0:
                    for b in range(blocks):
                        here[b] = opening * inbox[b, 0:SUB]
                        finish(b, opening * residuals[b])
                else:
                    apply_operator(lambda b, here=here: here[b], finish)
            omega = along.get() / length.get()
            omegas.append(omega)
            if sweep + 1 < SWEEPS:
                for b in range(blocks):
                    base = start_of(b) - omega * changes[b]
                    bases[b] = base
                    directions[0, b] = opening * base
                    begin.add(base * base)
                began = begin.get()
            else:
                squares = jnp.maximum(began - omega * along.get(), 0.0)
        sweeps = [jnp.sqrt(began / total), jnp.sqrt(squares / total)]
        which = lax.broadcasted_iota(jnp.int32, (SUB, count), 0) + rank * SUB
        rms = jnp.where(tile_lane == which, sweeps[0], 0.0)
        rms = jnp.where(tile_lane == which + count // 2, sweeps[1], rms)
        rms = jnp.sum(rms, axis=0, keepdims=True)
        for b in range(blocks):
            solved[b, 0:SUB] = omegas[0] * corrections[0, b] + omegas[1] * corrections[1, b]
            solved[b, SUB : SUB + 1] = rms
        for o in range(1, leaders):
            reply(place_of(lax.rem(rank + o, leaders))).start()
        for g in range(groups):
            for r in range(heads, rowcount):
                reply(g * rowcount + r).start()
        answers[rank] = solved[me]

    def await_reply(t):
        pltpu.make_async_remote_copy(
            src_ref=solved.at[0], dst_ref=answers.at[t],
            send_sem=back_send.at[0], recv_sem=back_recv.at[t],
            device_id=leader(t), device_id_type=MESH,
        ).wait_recv()

    for o in range(1, leaders):
        await_reply(lax.rem(rank + o, leaders))

    @pl.when(jnp.logical_not(leading))
    def _():
        await_reply(lax.rem(rank, leaders))

    whole = jnp.concatenate([answers[t, 0:SUB] for t in range(leaders)], axis=0)
    whole = jnp.concatenate(thirds(whole), axis=0)
    whole = lax.dot_general(
        whole, order[...], (((1,), (1,)), ((), ())), preferred_element_type=jnp.float32
    )
    packed_ref[0:nrhs] = added([whole[k * nrhs : (k + 1) * nrhs] for k in range(3)])
    line = answers[0, SUB : SUB + 1]
    for t in range(1, leaders):
        line = line + answers[t, SUB : SUB + 1]
    packed_ref[nrhs : nrhs + SUB] = jnp.concatenate(
        [line, turned(line, count // 2), jnp.zeros((SUB - 2, count), jnp.float32)], axis=0
    )

    for o in range(1, leaders):
        post(o).wait_send()

    @pl.when(jnp.logical_not(leading))
    def _():
        post(0).wait_send()

    @pl.when(leading)
    def _():
        for o in range(1, blocks):
            reply(lax.rem(me + o, blocks)).wait_send()


def unpack(packed_ref, out_ref, rms_ref):
    nrhs = out_ref.shape[0]
    out_ref[...] = packed_ref[:nrhs]
    rms_ref[...] = packed_ref[nrhs : nrhs + SWEEPS, :nrhs]


def whole_sweeps(groups, rowcount, right_side, links, coefs, reaction):
    nrhs, count = right_side.shape
    leaders = nrhs // SUB
    blocks = groups * rowcount
    dma = pltpu.SemaphoreType.DMA
    vmem = pl.BlockSpec(memory_space=pltpu.VMEM)

    def space(*shape):
        return pltpu.VMEM(shape, jnp.float32)

    packed = pl.pallas_call(
        functools.partial(kernel, groups, rowcount, count * groups * rowcount),
        out_shape=jax.ShapeDtypeStruct((nrhs + SUB, count), jnp.float32),
        in_specs=[vmem] * 4,
        out_specs=vmem,
        scratch_shapes=[
            space(leaders, SUB + 2, count), space(blocks, SUB + 2, count),
            space(leaders, SUB + 1, count), space(blocks, SUB + 1, count),
            space(13, blocks, count), space(count, count),
            space(blocks, SUB, count), space(blocks, SUB, count), space(2, blocks, SUB, count),
            space(SWEEPS, blocks, SUB, count), space(blocks, SUB, count), space(SUB, count),
            dma((leaders,)), dma((blocks,)), dma((blocks,)), dma((leaders,)),
        ],
        compiler_params=pltpu.CompilerParams(collective_id=0, has_side_effects=True),
    )(right_side, links, coefs.reshape(1, count), reaction.reshape(1, count))
    return pl.pallas_call(
        unpack,
        out_shape=(
            jax.ShapeDtypeStruct((nrhs, count), jnp.float32),
            jax.ShapeDtypeStruct((SWEEPS, nrhs), jnp.float32),
        ),
        in_specs=[vmem],
        out_specs=(vmem, vmem),
    )(packed)


def in_one_kernel(mesh):
    return mesh.shape["grp"] == 2 and 2 * SUB <= mesh.shape["row"] <= 4 * SUB


def solution(mesh):
    body = on_device
    if in_one_kernel(mesh):
        body = functools.partial(whole_sweeps, mesh.shape["grp"], mesh.shape["row"])
    return jax.shard_map(
        body,
        mesh=mesh,
        in_specs=(
            P(None, ("grp", "row")),
            P(None, ("grp", "row")),
            P(("grp", "row")),
            P(("grp", "row")),
        ),
        out_specs=(P(None, ("grp", "row")), P()),
        check_vma=False,
    )
```

time: 30.9 us -> 28.6 us (0.926)
  Pallas kernels: 30 us -> 27.7 us
    pallas_call x1, Pallas kernels: 28.6 us -> 26.3 us  [whole_sweeps(): pl.pallas_call(functools.partial(kernel, groups, rowcount, count * groups...]
where the time goes in v1:
time: 28.6 us; the launch traced here: 28.4 us
  Pallas kernels  27.7 us (97%)
  between operations  0.64 us (2%)
    pallas_call x1, Pallas kernels, whole_sweeps(): pl.pallas_call(functools.partial(kernel, groups, rowcount, count * groups...  26.3 us
    pallas_call x1, Pallas kernels, whole_sweeps(): pl.pallas_call(unpack, out_shape=(jax.ShapeDtypeStruct((nrhs, count), jnp...  1.39 us

profile of v1, /device:TPU:0, one launch (start us, length us, event | category | flops | bytes accessed | tf_op | source)
XLA Modules:
  0.0 28.4 jit_solution(14163991297044495057)
XLA Ops:
  0.6 26.3 %shard_map.59.packed_ref = f32[72,128]{1,0:T(8,128)} custom-call(f32[64,128]{1,0:T(8,128)} %right_ref.1, s32[8,128]{1,0:T(8,128)} %links_ref.1, f32[1,128]{1,0:T(1,128)} %bitcast.2, f32[1,128]{1,0:T(1,128)} %bitcast.3), custom_call_target="tpu_custom_call" | custom-call | tf_op jit(solution)/shard_map/pallas_call | solution.py:480
  27.0 1.4 %shard_map.60 = (f32[64,128]{1,0:T(8,128)}, f32[2,64]{1,0:T(2,128)}) custom-call(f32[72,128]{1,0:T(8,128)} %shard_map.59.packed_ref), custom_call_target="tpu_custom_call" | custom-call | tf_op jit(solution)/shard_map/pallas_call | solution.py:495

commit v2 on v1

v2 whole, which is shorter than its diff:
```python
import functools
import math

import jax
import jax.numpy as jnp
import numpy as np
from jax import lax
from jax.experimental import pallas as pl
from jax.experimental.pallas import tpu as pltpu
from jax.sharding import PartitionSpec as P

SWEEPS = 2
DEGREE = 4
CX, CY, CZ = 4, 2, 16
SUB, LANES = 8, 128
MESH = pl.DeviceIdType.MESH
HIGHEST = lax.Precision.HIGHEST


def shifted(block, axis, distance):
    devices = range(lax.axis_size(axis))
    route = [((i - distance) % len(devices), i) for i in devices]
    return lax.ppermute(block, axis, route)


def element_matrix():
    node_ids = np.arange(8)
    corner = np.stack([node_ids % 2, node_ids // 2 % 2, node_ids // 4], axis=1)
    gauss_points = np.array([0.5 - 0.5 / math.sqrt(3.0), 0.5 + 0.5 / math.sqrt(3.0)])
    stiffness = np.zeros((8, 8))
    for q in range(8):
        quad_point = gauss_points[np.array([q % 2, q // 2 % 2, q // 4])]
        values = np.where(corner > 0.5, quad_point, 1.0 - quad_point)
        slopes = np.where(corner > 0.5, 1.0, -1.0)
        gradient = np.stack(
            [
                slopes[:, 0] * values[:, 1] * values[:, 2],
                values[:, 0] * slopes[:, 1] * values[:, 2],
                values[:, 0] * values[:, 1] * slopes[:, 2],
            ],
            axis=1,
        )
        stiffness = stiffness + gradient @ gradient.T / 8.0
    return stiffness


def element_images(window, offsets, weights, stiffness):
    corners = window[:, offsets]
    images = (
        jnp.einsum("ml,rle->rme", stiffness, corners, precision=lax.Precision.HIGHEST) * weights
    )
    return jnp.zeros_like(window).at[:, offsets].add(images)


def on_device(right_side, links, coefs, reaction):
    stiffness = jnp.asarray(element_matrix(), dtype=jnp.float32)
    count = right_side.shape[1]
    groups = lax.axis_size("grp")
    rowcount = lax.axis_size("row")
    group_id = lax.axis_index("grp")
    row_id = lax.axis_index("row")
    total = count * groups * rowcount
    owner = links // count
    slot = links % count
    first = jnp.mod(owner // rowcount - group_id, groups)
    second = jnp.mod(owner % rowcount - row_id, rowcount)
    offsets = (first * 2 + second) * count + slot

    def apply_operator(field):
        above_row = shifted(field, "row", -1)
        upper = shifted(jnp.stack([field, above_row], axis=0), "grp", -1)
        window = jnp.concatenate([field, above_row, upper[0], upper[1]], axis=1)
        summed = element_images(window, offsets, coefs, stiffness)
        back = shifted(
            jnp.stack([summed[:, 2 * count : 3 * count], summed[:, 3 * count :]], axis=0), "grp", 1
        )
        first_col = summed[:, :count] + back[0]
        second_col = summed[:, count : 2 * count] + back[1]
        first_col = first_col + shifted(second_col, "row", 1)
        return first_col + reaction * field

    image = apply_operator(right_side)
    cross, square = lax.psum(
        (jnp.sum(right_side * image, axis=1), jnp.sum(image * image, axis=1)), ("grp", "row")
    )
    theta = square / cross
    upper = (1.5 * theta)[:, None]
    lower = upper / 10.0
    center = (upper + lower) / 2.0
    half = (upper - lower) / 2.0
    sigma = center / half
    solution = jnp.zeros_like(right_side)
    residual = right_side
    history = []
    for sweep in range(SWEEPS):
        start = residual
        correction = jnp.zeros_like(right_side)
        rho_now = 1.0 / sigma
        direction = residual / center
        for step in range(DEGREE):
            correction = correction + direction
            residual = residual - apply_operator(direction)
            if step + 1 < DEGREE:
                rho_next = 1.0 / (2.0 * sigma - rho_now)
                direction = rho_next * rho_now * direction + 2.0 * rho_next / half * residual
                rho_now = rho_next
        change = start - residual
        along, length, begin = lax.psum(
            (
                jnp.sum(start * change, axis=1),
                jnp.sum(change * change, axis=1),
                jnp.sum(start * start, axis=1),
            ),
            ("grp", "row"),
        )
        omega = along / length
        residual = start - omega[:, None] * change
        squares = begin - 2.0 * omega * along + omega * omega * length
        solution = solution + omega[:, None] * correction
        history.append(jnp.sqrt(squares / total))
    return (solution, jnp.stack(history, axis=0))


def thirds(a):
    high = a.astype(jnp.bfloat16).astype(jnp.float32)
    rest = a - high
    middle = rest.astype(jnp.bfloat16).astype(jnp.float32)
    return [high, middle, rest - middle]


def added(parts):
    high, middle, low = parts
    return high + middle + low


def turned(a, distance, axis=1):
    return pltpu.roll(a, distance % a.shape[axis], axis)


def tile_iota(axis):
    return lax.broadcasted_iota(jnp.int32, (SUB, LANES), axis)


def exchanged(tile):
    sub, low = tile_iota(0), tile_iota(1)
    for bit in (1, 2, 4):
        rise = turned(turned(tile, -bit, 0), bit)
        fall = turned(turned(tile, bit, 0), -bit)
        in_low, in_sub = low // bit % 2, sub // bit % 2
        tile = jnp.where(in_low > in_sub, rise, jnp.where(in_low < in_sub, fall, tile))
    return tile


def paired(first, second):
    top = tile_iota(0) < SUB // 2
    return (
        jnp.where(top, first, turned(second, SUB // 2, 0)),
        jnp.where(top, turned(first, SUB // 2, 0), second),
    )


def chebyshev_steps():
    sigma = (1.5 + 0.15) / (1.5 - 0.15)
    rho_now = 1.0 / sigma
    steps = []
    for _ in range(DEGREE - 1):
        rho_next = 1.0 / (2.0 * sigma - rho_now)
        steps.append((rho_next * rho_now, 2.0 * rho_next / ((1.5 - 0.15) / 2.0)))
        rho_now = rho_next
    return 2.0 / (1.5 + 0.15), steps


class Total:
    def __init__(self):
        self.parts = [None] * 4
        self.at = 0

    def add(self, value):
        k = self.at % 4
        self.parts[k] = value if self.parts[k] is None else self.parts[k] + value
        self.at += 1

    def folded(self):
        a, b, c, d = self.parts
        value = (a + b) + (c + d)
        for bit in (4, 2, 1):
            value = value + turned(value, bit, 0)
        return value


def over_z(value):
    parts = [value] + [turned(value, SUB * k) for k in range(1, LANES // SUB)]
    while len(parts) > 1:
        parts = [a + b for a, b in zip(parts[::2], parts[1::2])]
    return parts[0]


def summed(first, second):
    top = tile_iota(0) < SUB // 2
    both = over_z(jnp.where(top, first.folded(), second.folded()))
    other = turned(both, SUB // 2, 0)
    return jnp.where(top, both, other), jnp.where(top, other, both)


def kernel(
    groups, rowcount, total,
    right_hbm, links_hbm, coefs_hbm, react_hbm,
    packed_ref,
    right_ref, links_ref, coefs_ref, react_ref,
    auxout, auxin, outbox, inbox, answers, solved, order, spread, wide,
    masses, masses_z, lows, lows_z, boths, boths_z, diag,
    bases, changes, directions, corrections, residuals,
    in_sem, aux_send, aux_recv, out_send, out_recv, back_send, back_recv,
):
    nrhs, count = right_ref.shape
    leaders = nrhs // SUB
    heads = leaders // groups
    blocks = groups * rowcount
    planes = rowcount * CY
    grp = lax.axis_index("grp")
    row = lax.axis_index("row")
    me = grp * rowcount + row
    leading = row < heads
    rank = grp * heads + row

    def leader(t):
        return (t // heads, lax.rem(t, heads))

    def block(b):
        return (b // rowcount, lax.rem(b, rowcount))

    def place_of(t):
        return (t // heads) * rowcount + lax.rem(t, heads)

    barrier = pltpu.get_barrier_semaphore()

    @pl.when(leading)
    def _():
        far = sorted(range(1, blocks), key=lambda o: -min(o % rowcount, rowcount - o % rowcount))
        for o in far:
            pl.semaphore_signal(
                barrier, inc=1, device_id=block(lax.rem(me + o, blocks)), device_id_type=MESH
            )

    loads = [
        pltpu.make_async_copy(source, target, in_sem.at[k])
        for k, (source, target) in enumerate(
            [(links_hbm, links_ref), (coefs_hbm, coefs_ref), (react_hbm, react_ref), (right_hbm, right_ref)]
        )
    ]
    for load in loads:
        load.start()

    lane = lax.broadcasted_iota(jnp.int32, (count, count), 1)
    down = lax.broadcasted_iota(jnp.int32, (count, count), 0)
    element = ((lane % CX) * CY + lane // CX % CY) * CZ + lane // SUB
    to_lanes = (down == element).astype(jnp.float32)
    same_z = (down // SUB == lane // SUB).astype(jnp.float32)
    spread[0:count] = same_z
    spread[count : 2 * count] = same_z

    for load in loads[:3]:
        load.wait()
    slots = (links_ref[0:1, :] - me * count).astype(jnp.float32)
    mass = thirds(coefs_ref[...] * (-1.0 / 12.0))
    small = jnp.concatenate([slots] + mass + [jnp.zeros((SUB - 4, count), jnp.float32)], axis=0)
    small = jnp.dot(small, to_lanes, preferred_element_type=jnp.float32)
    mass = added([small[k : k + 1] for k in (1, 2, 3)])
    order[...] = (down.astype(jnp.float32) == small[0:1]).astype(jnp.float32)
    react = thirds(react_ref[...])
    react = jnp.concatenate(react + [jnp.zeros((SUB - 3, count), jnp.float32)], axis=0)
    loads[3].wait()
    stack = jnp.concatenate([react] + thirds(right_ref[...]), axis=0)
    stack = jnp.dot(stack, order[...], preferred_element_type=jnp.float32)
    react = added([stack[k : k + 1] for k in range(3)])
    auxout[...] = jnp.concatenate([mass, react], axis=0)
    field = added([stack[SUB + k * nrhs : SUB + (k + 1) * nrhs] for k in range(3)])

    def post(o, source, target, send, recv):
        t = lax.rem(rank + o, leaders)
        return pltpu.make_async_remote_copy(
            src_ref=source(t), dst_ref=target.at[me], send_sem=send.at[t], recv_sem=recv,
            device_id=leader(t), device_id_type=MESH,
        )

    def post_aux(o):
        return post(o, lambda t: auxout, auxin, aux_send, aux_recv.at[me])

    def post_field(o):
        return post(o, lambda t: outbox.at[t], inbox, out_send, out_recv.at[me])

    for t in range(leaders):
        outbox[t] = exchanged(field[t * SUB : (t + 1) * SUB])
    pl.semaphore_wait(barrier, jnp.where(leading, leaders - 1, leaders))

    for send in (post_aux, post_field):
        for o in range(1, leaders):
            send(o).start()

        @pl.when(jnp.logical_not(leading))
        def _(send=send):
            send(0).start()

    def reply(b):
        return pltpu.make_async_remote_copy(
            src_ref=solved.at[b], dst_ref=answers.at[rank],
            send_sem=back_send.at[b], recv_sem=back_recv.at[rank],
            device_id=block(b), device_id_type=MESH,
        )

    @pl.when(leading)
    def _():
        auxin[me] = auxout[...]
        for o in range(1, blocks):
            b = lax.rem(me + o, blocks)
            pltpu.make_async_remote_copy(
                src_ref=auxout, dst_ref=auxin.at[b],
                send_sem=aux_send.at[0], recv_sem=aux_recv.at[b],
                device_id=block(b), device_id_type=MESH,
            ).wait_recv()

        own = tile_iota(1) % SUB == tile_iota(0)
        for k in range(2):
            high, middle, _ = thirds(auxin[:, k, :])
            wide[0, k * blocks : (k + 1) * blocks] = high
            wide[1, k * blocks : (k + 1) * blocks] = middle
        pieces = [
            jnp.concatenate(
                [jnp.where(own, wide[part, k : k + 1, :], 0.0) for k in range(2 * blocks)], axis=0
            )
            for part in range(2)
        ]
        tiles = jnp.dot(
            jnp.concatenate(pieces, axis=1), spread[...], preferred_element_type=jnp.float32
        )
        tiles = [tiles[k * SUB : (k + 1) * SUB] for k in range(2 * blocks)]
        for q in range(rowcount):
            for k, m in enumerate(paired(tiles[q], tiles[rowcount + q])):
                y = CY * q + k
                m_z = turned(m, SUB)
                low, low_z = turned(m, 1, 0), turned(m_z, 1, 0)
                masses[y], masses_z[y] = m, m_z
                lows[y], lows_z[y] = low, low_z
                boths[y], boths_z[y] = m + low, m_z + low_z
        for q in range(rowcount):
            reacts = paired(tiles[blocks + q], tiles[blocks + rowcount + q])
            for k, react in enumerate(reacts):
                y = CY * q + k
                around = (boths[y] + boths_z[y]) + (boths[(y - 1) % planes] + boths_z[(y - 1) % planes])
                diag[y] = react - 4.0 * around

        inbox[me] = outbox[rank]
        for o in range(1, blocks):
            b = lax.rem(me + o, blocks)
            pltpu.make_async_remote_copy(
                src_ref=outbox.at[0], dst_ref=inbox.at[b],
                send_sem=out_send.at[0], recv_sem=out_recv.at[b],
                device_id=block(b), device_id_type=MESH,
            ).wait_recv()
        for q in range(rowcount):
            for k, value in enumerate(paired(inbox[q], inbox[rowcount + q])):
                bases[0, CY * q + k] = value

        def apply_operator(source, sink):
            taken = {}

            def around(y):
                y = y % planes
                if y not in taken:
                    v = source(y)
                    above, below = turned(v, -SUB), turned(v, SUB)
                    taken[y] = (v, above, below, v + above, v + below)
                return taken[y]

            for y in range(planes):
                v, above, below, _, _ = around(y)
                _, next_above, next_below, next_up, next_down = around(y + 1)
                _, last_above, last_below, last_up, last_down = around(y - 1)
                sides = [above + next_up, below + next_down, above + last_up, below + last_down]
                diagonal = [next_above, next_below, last_above, last_below]

                def weighed(a, b, values, y=y):
                    z = (y - 1) % planes
                    products = [
                        c * value for c, value in zip((a[y], b[y], a[z], b[z]), values)
                    ]
                    return (products[0] + products[1]) + (products[2] + products[3])

                ahead = turned(weighed(lows, lows_z, sides), -1, 0)
                behind = turned(weighed(masses, masses_z, sides), 1, 0)
                middle = weighed(boths, boths_z, diagonal) + diag[y] * v
                sink(y, middle + (ahead + behind))

        scale, steps = chebyshev_steps()
        square, cross = Total(), Total()

        def first_image(y, image):
            residuals[y] = image
            square.add(image * image)
            cross.add(bases[0, y] * image)

        apply_operator(lambda y: bases[0, y], first_image)
        square, cross = summed(square, cross)
        inverse = cross / square
        opening = scale * inverse

        omegas, squares = [], []
        for sweep in range(SWEEPS):
            along, length, begin = Total(), Total(), Total()
            for step in range(DEGREE):
                here, there = directions.at[step % 2], directions.at[(step + 1) % 2]

                def finish(y, image, step=step, here=here, there=there, sweep=sweep):
                    residual = (bases[sweep, y] if step == 0 else residuals[y]) - image
                    if step + 1 < DEGREE:
                        direction = here[y]
                        keep, gain = steps[step]
                        following = keep * direction + (gain * inverse) * residual
                        residuals[y] = residual
                        there[y] = following
                        so_far = direction if step == 0 else corrections[sweep, y]
                        corrections[sweep, y] = so_far + following
                    else:
                        start = bases[sweep, y]
                        change = start - residual
                        changes[y] = change
                        along.add(start * change)
                        length.add(change * change)

                if sweep == 0 and step == 0:
                    for y in range(planes):
                        here[y] = opening * bases[0, y]
                        finish(y, opening * residuals[y])
                else:
                    apply_operator(lambda y, here=here: here[y], finish)
            along, length = summed(along, length)
            omega = along / length
            omegas.append(omega)
            if sweep + 1 < SWEEPS:
                for y in range(planes):
                    base = bases[sweep, y] - omega * changes[y]
                    bases[sweep + 1, y] = base
                    directions[0, y] = opening * base
                    begin.add(base * base)
                began = over_z(begin.folded())
        group = tile_iota(1) // SUB
        last = jnp.maximum(began - omega * along, 0.0)
        rms = jnp.where(group == rank, began, jnp.where(group == rank + leaders, last, 0.0))
        rms = jnp.sqrt(rms / total)[0:1]
        for q in range(rowcount):
            values = [
                omegas[0] * corrections[0, CY * q + k] + omegas[1] * corrections[1, CY * q + k]
                for k in range(CY)
            ]
            for p, tile in enumerate(paired(*values)):
                solved[p * rowcount + q, 0:SUB] = tile
                solved[p * rowcount + q, SUB : SUB + 1] = rms
        for o in range(1, leaders):
            reply(place_of(lax.rem(rank + o, leaders))).start()
        for g in range(groups):
            for r in range(heads, rowcount):
                reply(g * rowcount + r).start()
        answers[rank] = solved[me]

    def await_reply(t):
        pltpu.make_async_remote_copy(
            src_ref=solved.at[0], dst_ref=answers.at[t],
            send_sem=back_send.at[0], recv_sem=back_recv.at[t],
            device_id=leader(t), device_id_type=MESH,
        ).wait_recv()

    for o in range(1, leaders):
        await_reply(lax.rem(rank + o, leaders))

    @pl.when(jnp.logical_not(leading))
    def _():
        await_reply(lax.rem(rank, leaders))

    whole = jnp.concatenate([exchanged(answers[t, 0:SUB]) for t in range(leaders)], axis=0)
    whole = jnp.concatenate(thirds(whole), axis=0)
    whole = lax.dot_general(
        whole, order[...], (((1,), (1,)), ((), ())), preferred_element_type=jnp.float32
    )
    packed_ref[0:nrhs] = added([whole[k * nrhs : (k + 1) * nrhs] for k in range(3)])
    line = answers[0, SUB : SUB + 1]
    for t in range(1, leaders):
        line = line + answers[t, SUB : SUB + 1]
    packed_ref[nrhs : nrhs + SUB] = jnp.concatenate(
        [line, turned(line, count // 2), jnp.zeros((SUB - 2, count), jnp.float32)], axis=0
    )

    for send in (post_aux, post_field):
        for o in range(1, leaders):
            send(o).wait_send()

        @pl.when(jnp.logical_not(leading))
        def _(send=send):
            send(0).wait_send()

    @pl.when(leading)
    def _():
        for o in range(1, blocks):
            reply(lax.rem(me + o, blocks)).wait_send()


def unpack(packed_ref, out_ref, rms_ref):
    nrhs = out_ref.shape[0]
    out_ref[...] = packed_ref[:nrhs]
    rms_ref[...] = packed_ref[nrhs : nrhs + SWEEPS, :nrhs]


def whole_sweeps(groups, rowcount, right_side, links, coefs, reaction):
    nrhs, count = right_side.shape
    leaders = nrhs // SUB
    blocks = groups * rowcount
    planes = rowcount * CY
    dma = pltpu.SemaphoreType.DMA
    vmem = pl.BlockSpec(memory_space=pltpu.VMEM)

    def space(*shape):
        return pltpu.VMEM(shape, jnp.float32)

    plane = space(planes, SUB, count)
    twice = space(SWEEPS, planes, SUB, count)
    packed = pl.pallas_call(
        functools.partial(kernel, groups, rowcount, count * groups * rowcount),
        out_shape=jax.ShapeDtypeStruct((nrhs + SUB, count), jnp.float32),
        in_specs=[pl.BlockSpec(memory_space=pl.ANY)] * 4,
        out_specs=vmem,
        scratch_shapes=[
            space(nrhs, count), pltpu.VMEM(links.shape, jnp.int32), space(1, count), space(1, count),
            space(2, count), space(blocks, 2, count),
            space(leaders, SUB, count), space(blocks, SUB, count),
            space(leaders, SUB + 1, count), space(blocks, SUB + 1, count),
            space(count, count), space(2 * count, count), space(2, 2 * blocks, count),
            plane, plane, plane, plane, plane, plane, plane,
            twice, plane, space(2, planes, SUB, count), twice, plane,
            dma((4,)), dma((leaders,)), dma((blocks,)), dma((leaders,)), dma((blocks,)),
            dma((blocks,)), dma((leaders,)),
        ],
        compiler_params=pltpu.CompilerParams(collective_id=0, has_side_effects=True),
    )(right_side, links, coefs.reshape(1, count), reaction.reshape(1, count))
    return pl.pallas_call(
        unpack,
        out_shape=(
            jax.ShapeDtypeStruct((nrhs, count), jnp.float32),
            jax.ShapeDtypeStruct((SWEEPS, nrhs), jnp.float32),
        ),
        in_specs=[vmem],
        out_specs=(vmem, vmem),
    )(packed)


def in_one_kernel(mesh):
    return mesh.shape["grp"] == SUB // CX and 2 * SUB <= mesh.shape["row"] <= 4 * SUB


def solution(mesh):
    body = on_device
    if in_one_kernel(mesh):
        body = functools.partial(whole_sweeps, mesh.shape["grp"], mesh.shape["row"])
    return jax.shard_map(
        body,
        mesh=mesh,
        in_specs=(
            P(None, ("grp", "row")),
            P(None, ("grp", "row")),
            P(("grp", "row")),
            P(("grp", "row")),
        ),
        out_specs=(P(None, ("grp", "row")), P()),
        check_vma=False,
    )
```

time: 28.6 us -> 19.7 us (0.69)
  Pallas kernels: 27.7 us -> 18.8 us
    pallas_call x1, Pallas kernels: 26.3 us -> 17.4 us  [whole_sweeps(): pl.pallas_call(functools.partial(kernel, groups, rowcount, count * groups...]
where the time goes in v2:
time: 19.7 us; the launch traced here: 19.4 us
  Pallas kernels  18.8 us (95%)
  between operations  0.64 us (3%)
    pallas_call x1, Pallas kernels, whole_sweeps(): pl.pallas_call(functools.partial(kernel, groups, rowcount, count * groups...  17.4 us
    pallas_call x1, Pallas kernels, whole_sweeps(): pl.pallas_call(unpack, out_shape=(jax.ShapeDtypeStruct((nrhs, count), jnp...  1.39 us

profile of v2, /device:TPU:0, one launch (start us, length us, event | category | flops | bytes accessed | tf_op | source)
XLA Modules:
  0.0 19.4 jit_solution(17852316292906992607)
XLA Ops:
  0.6 17.4 %shard_map.59.packed_ref = f32[72,128]{1,0:T(8,128)} custom-call(f32[64,128]{1,0:T(8,128)} %right_hbm.1, s32[8,128]{1,0:T(8,128)} %links_hbm.1, f32[1,128]{1,0:T(1,128)} %bitcast.2, f32[1,128]{1,0:T(1,128)} %bitcast.3), custom_call_target="tpu_custom_call" | custom-call | tf_op jit(solution)/shard_map/pallas_call | solution.py:525
  18.0 1.4 %shard_map.60 = (f32[64,128]{1,0:T(8,128)}, f32[2,64]{1,0:T(2,128)}) custom-call(f32[72,128]{1,0:T(8,128)} %shard_map.59.packed_ref), custom_call_target="tpu_custom_call" | custom-call | tf_op jit(solution)/shard_map/pallas_call | solution.py:543

commit v3 on v2

--- a/solution.py
+++ b/solution.py
@@ -143,11 +143,14 @@
 
 def exchanged(tile):
     sub, low = tile_iota(0), tile_iota(1)
-    for bit in (1, 2, 4):
-        rise = turned(turned(tile, -bit, 0), bit)
-        fall = turned(turned(tile, bit, 0), -bit)
-        in_low, in_sub = low // bit % 2, sub // bit % 2
-        tile = jnp.where(in_low > in_sub, rise, jnp.where(in_low < in_sub, fall, tile))
+    for unit, radix in ((1, 4), (4, 2)):
+        ahead = low // unit % radix - sub // unit % radix
+        result = tile
+        for k in range(1 - radix, radix):
+            if k:
+                moved = turned(turned(tile, -k * unit, 0), k * unit)
+                result = jnp.where(ahead == k, moved, result)
+        tile = result
     return tile
 
 
@@ -205,7 +208,7 @@
 def kernel(
     groups, rowcount, total,
     right_hbm, links_hbm, coefs_hbm, react_hbm,
-    packed_ref,
+    solution_ref, rms_ref,
     right_ref, links_ref, coefs_ref, react_ref,
     auxout, auxin, outbox, inbox, answers, solved, order, spread, wide,
     masses, masses_z, lows, lows_z, boths, boths_z, diag,
@@ -236,11 +239,14 @@
 
     @pl.when(leading)
     def _():
-        far = sorted(range(1, blocks), key=lambda o: -min(o % rowcount, rowcount - o % rowcount))
-        for o in far:
-            pl.semaphore_signal(
-                barrier, inc=1, device_id=block(lax.rem(me + o, blocks)), device_id_type=MESH
-            )
+        def nearness(place):
+            d, o = place
+            return abs(2 * o - rowcount) - 2 * heads * d - heads * (o % heads == heads // 2)
+
+        peers = [(d, o) for d in range(groups) for o in range(rowcount) if d or o]
+        for d, o in sorted(peers, key=nearness):
+            peer = (lax.rem(grp + d, groups), lax.rem(row + o, rowcount))
+            pl.semaphore_signal(barrier, inc=1, device_id=peer, device_id_type=MESH)
 
     loads = [
         pltpu.make_async_copy(source, target, in_sem.at[k])
@@ -253,20 +259,20 @@
 
     lane = lax.broadcasted_iota(jnp.int32, (count, count), 1)
     down = lax.broadcasted_iota(jnp.int32, (count, count), 0)
-    element = ((lane % CX) * CY + lane // CX % CY) * CZ + lane // SUB
-    to_lanes = (down == element).astype(jnp.float32)
     same_z = (down // SUB == lane // SUB).astype(jnp.float32)
     spread[0:count] = same_z
     spread[count : 2 * count] = same_z
+    low = tile_iota(1)
+    element = ((low % CX) * CY + low // CX % CY) * CZ + low // SUB
+
+    def to_lanes(line):
+        return jnp.take_along_axis(jnp.broadcast_to(line, (SUB, count)), element, axis=1)[0:1]
 
     for load in loads[:3]:
         load.wait()
-    slots = (links_ref[0:1, :] - me * count).astype(jnp.float32)
-    mass = thirds(coefs_ref[...] * (-1.0 / 12.0))
-    small = jnp.concatenate([slots] + mass + [jnp.zeros((SUB - 4, count), jnp.float32)], axis=0)
-    small = jnp.dot(small, to_lanes, preferred_element_type=jnp.float32)
-    mass = added([small[k : k + 1] for k in (1, 2, 3)])
-    order[...] = (down.astype(jnp.float32) == small[0:1]).astype(jnp.float32)
+    slots = to_lanes(links_ref[0:1, :] - me * count)
+    order[...] = (down == slots).astype(jnp.float32)
+    mass = to_lanes(coefs_ref[...] * (-1.0 / 12.0))
     react = thirds(react_ref[...])
     react = jnp.concatenate(react + [jnp.zeros((SUB - 3, count), jnp.float32)], axis=0)
     loads[3].wait()
@@ -481,13 +487,12 @@
     whole = lax.dot_general(
         whole, order[...], (((1,), (1,)), ((), ())), preferred_element_type=jnp.float32
     )
-    packed_ref[0:nrhs] = added([whole[k * nrhs : (k + 1) * nrhs] for k in range(3)])
+    solution_ref[...] = added([whole[k * nrhs : (k + 1) * nrhs] for k in range(3)])
     line = answers[0, SUB : SUB + 1]
     for t in range(1, leaders):
         line = line + answers[t, SUB : SUB + 1]
-    packed_ref[nrhs : nrhs + SUB] = jnp.concatenate(
-        [line, turned(line, count // 2), jnp.zeros((SUB - 2, count), jnp.float32)], axis=0
-    )
+    other = turned(line, count // 2)
+    rms_ref[...] = jnp.concatenate([line, other], axis=0)[:, :nrhs]
 
     for send in (post_aux, post_field):
         for o in range(1, leaders):
@@ -503,10 +508,15 @@
             reply(lax.rem(me + o, blocks)).wait_send()
 
 
-def unpack(packed_ref, out_ref, rms_ref):
-    nrhs = out_ref.shape[0]
-    out_ref[...] = packed_ref[:nrhs]
-    rms_ref[...] = packed_ref[nrhs : nrhs + SWEEPS, :nrhs]
+def write_out(solution_ref, rms_ref, out_hbm, rms_hbm, sems):
+    copies = [
+        pltpu.make_async_copy(solution_ref, out_hbm, sems.at[0]),
+        pltpu.make_async_copy(rms_ref, rms_hbm, sems.at[1]),
+    ]
+    for copy in copies:
+        copy.start()
+    for copy in copies:
+        copy.wait()
 
 
 def whole_sweeps(groups, rowcount, right_side, links, coefs, reaction):
@@ -522,11 +532,11 @@
 
     plane = space(planes, SUB, count)
     twice = space(SWEEPS, planes, SUB, count)
-    packed = pl.pallas_call(
+    found = pl.pallas_call(
         functools.partial(kernel, groups, rowcount, count * groups * rowcount),
-        out_shape=jax.ShapeDtypeStruct((nrhs + SUB, count), jnp.float32),
+        out_shape=(pltpu.VMEM((nrhs, count), jnp.float32), pltpu.VMEM((SWEEPS, nrhs), jnp.float32)),
         in_specs=[pl.BlockSpec(memory_space=pl.ANY)] * 4,
-        out_specs=vmem,
+        out_specs=(vmem, vmem),
         scratch_shapes=[
             space(nrhs, count), pltpu.VMEM(links.shape, jnp.int32), space(1, count), space(1, count),
             space(2, count), space(blocks, 2, count),
@@ -541,14 +551,15 @@
         compiler_params=pltpu.CompilerParams(collective_id=0, has_side_effects=True),
     )(right_side, links, coefs.reshape(1, count), reaction.reshape(1, count))
     return pl.pallas_call(
-        unpack,
+        write_out,
         out_shape=(
             jax.ShapeDtypeStruct((nrhs, count), jnp.float32),
             jax.ShapeDtypeStruct((SWEEPS, nrhs), jnp.float32),
         ),
-        in_specs=[vmem],
-        out_specs=(vmem, vmem),
-    )(packed)
+        in_specs=[vmem, vmem],
+        out_specs=[pl.BlockSpec(memory_space=pl.ANY)] * 2,
+        scratch_shapes=[dma((2,))],
+    )(*[pltpu.with_memory_space_constraint(f, pltpu.VMEM) for f in found])
 
 
 def in_one_kernel(mesh):

time: 19.7 us -> 18.1 us (0.919)
  Pallas kernels: 18.8 us -> 17.2 us
    pallas_call x1, Pallas kernels: 17.4 us -> 16.6 us  [whole_sweeps(): pl.pallas_call(functools.partial(kernel, groups, rowcount, count * groups...]
    pallas_call x1, Pallas kernels: 1.39 us -> 0.64 us  [whole_sweeps(): pl.pallas_call(write_out, out_shape=(jax.ShapeDtypeStruct((nrhs, count),...]
where the time goes in v3:
time: 18.1 us; the launch traced here: 17.9 us
  Pallas kernels  17.2 us (95%)
  between operations  0.64 us (4%)
    pallas_call x1, Pallas kernels, whole_sweeps(): pl.pallas_call(functools.partial(kernel, groups, rowcount, count * groups...  16.6 us
    pallas_call x1, Pallas kernels, whole_sweeps(): pl.pallas_call(write_out, out_shape=(jax.ShapeDtypeStruct((nrhs, count),...  0.64 us

profile of v3, /device:TPU:0, one launch (start us, length us, event | category | flops | bytes accessed | tf_op | source)
XLA Modules:
  0.0 17.9 jit_solution(12186217701164459038)
XLA Ops:
  0.6 16.6 %shard_map.59 = (f32[64,128]{1,0:T(8,128)S(1)}, f32[2,64]{1,0:T(2,128)S(1)}) custom-call(f32[64,128]{1,0:T(8,128)} %right_hbm.1, s32[8,128]{1,0:T(8,128)} %links_hbm.1, f32[1,128]{1,0:T(1,128)} %bitcast.2, f32[1,128]{1,0:T(1,128)} %bitcast.3), custom_call_target="tpu_custom_call" | custom-call | tf_op jit(solution)/shard_map/pallas_call | solution.py:535
  17.2 0.6 %shard_map.60 = (f32[64,128]{1,0:T(8,128)}, f32[2,64]{1,0:T(2,128)}) custom-call(f32[64,128]{1,0:T(8,128)S(1)} %get-tuple-element.4.solution_ref, f32[2,64]{1,0:T(2,128)S(1)} %get-tuple-element.5.rms_ref), custom_call_target="tpu_custom_call" | custom-call | tf_op jit(solution)/shard_map/pallas_call | solution.py:553

commit v4 on v3

--- a/solution.py
+++ b/solution.py
@@ -162,15 +162,20 @@
     )
 
 
-def chebyshev_steps():
-    sigma = (1.5 + 0.15) / (1.5 - 0.15)
+def chebyshev_weights():
+    center, half = (1.5 + 0.15) / 2.0, (1.5 - 0.15) / 2.0
+    sigma = center / half
     rho_now = 1.0 / sigma
-    steps = []
-    for _ in range(DEGREE - 1):
+    direction, residual = np.zeros(DEGREE + 1), np.zeros(DEGREE + 1)
+    correction = np.zeros(DEGREE + 1)
+    residual[0], direction[0] = 1.0, 1.0 / center
+    for _ in range(DEGREE):
+        correction = correction + direction
+        residual = residual - np.roll(direction, 1)
         rho_next = 1.0 / (2.0 * sigma - rho_now)
-        steps.append((rho_next * rho_now, 2.0 * rho_next / ((1.5 - 0.15) / 2.0)))
+        direction = rho_next * rho_now * direction + 2.0 * rho_next / half * residual
         rho_now = rho_next
-    return 2.0 / (1.5 + 0.15), steps
+    return [float(b) for b in correction[:DEGREE]], [-float(c) for c in residual[1:]]
 
 
 class Total:
@@ -212,28 +217,33 @@
     right_ref, links_ref, coefs_ref, react_ref,
     auxout, auxin, outbox, inbox, answers, solved, order, spread, wide,
     masses, masses_z, lows, lows_z, boths, boths_z, diag,
-    bases, changes, directions, corrections, residuals,
+    bases, changes, corrections, powers, mixes,
     in_sem, aux_send, aux_recv, out_send, out_recv, back_send, back_recv,
 ):
     nrhs, count = right_ref.shape
     leaders = nrhs // SUB
-    heads = leaders // groups
+    near, second = leaders - CY, CY
     blocks = groups * rowcount
     planes = rowcount * CY
     grp = lax.axis_index("grp")
     row = lax.axis_index("row")
     me = grp * rowcount + row
-    leading = row < heads
-    rank = grp * heads + row
+    leading = row < jnp.where(grp == 0, near, second)
+    rank = jnp.where(grp == 0, row, near + row)
 
     def leader(t):
-        return (t // heads, lax.rem(t, heads))
+        if isinstance(t, int):
+            return (0, t) if t < near else (1, t - near)
+        return (jnp.where(t < near, 0, 1), jnp.where(t < near, t, t - near))
 
     def block(b):
         return (b // rowcount, lax.rem(b, rowcount))
 
     def place_of(t):
-        return (t // heads) * rowcount + lax.rem(t, heads)
+        return jnp.where(t < near, t, rowcount + t - near)
+
+    def another(k):
+        return jnp.where(k < rank, k, k + 1)
 
     barrier = pltpu.get_barrier_semaphore()
 
@@ -241,7 +251,7 @@
     def _():
         def nearness(place):
             d, o = place
-            return abs(2 * o - rowcount) - 2 * heads * d - heads * (o % heads == heads // 2)
+            return abs(2 * o - rowcount) - rowcount // 2 * d - CX * (o % CX == CX // 2)
 
         peers = [(d, o) for d in range(groups) for o in range(rowcount) if d or o]
         for d, o in sorted(peers, key=nearness):
@@ -282,30 +292,36 @@
     auxout[...] = jnp.concatenate([mass, react], axis=0)
     field = added([stack[SUB + k * nrhs : SUB + (k + 1) * nrhs] for k in range(3)])
 
-    def post(o, source, target, send, recv):
-        t = lax.rem(rank + o, leaders)
+    def post(t, source, target, send, recv):
         return pltpu.make_async_remote_copy(
             src_ref=source(t), dst_ref=target.at[me], send_sem=send.at[t], recv_sem=recv,
             device_id=leader(t), device_id_type=MESH,
         )
 
-    def post_aux(o):
-        return post(o, lambda t: auxout, auxin, aux_send, aux_recv.at[me])
-
-    def post_field(o):
-        return post(o, lambda t: outbox.at[t], inbox, out_send, out_recv.at[me])
+    def post_aux(t):
+        return post(t, lambda t: auxout, auxin, aux_send, aux_recv.at[me])
+
+    def post_field(t):
+        return post(t, lambda t: outbox.at[t], inbox, out_send, out_recv.at[me])
+
+    def each_post(act):
+        for send in (post_aux, post_field):
+
+            @pl.when(leading)
+            def _(send=send):
+                for k in range(leaders - 1):
+                    act(send(another(k)))
+
+            @pl.when(jnp.logical_not(leading))
+            def _(send=send):
+                for t in range(leaders):
+                    act(send(t))
 
     for t in range(leaders):
         outbox[t] = exchanged(field[t * SUB : (t + 1) * SUB])
     pl.semaphore_wait(barrier, jnp.where(leading, leaders - 1, leaders))
 
-    for send in (post_aux, post_field):
-        for o in range(1, leaders):
-            send(o).start()
-
-        @pl.when(jnp.logical_not(leading))
-        def _(send=send):
-            send(0).start()
+    each_post(lambda copy: copy.start())
 
     def reply(b):
         return pltpu.make_async_remote_copy(
@@ -314,61 +330,72 @@
             device_id=block(b), device_id_type=MESH,
         )
 
+    outside = [
+        (g, r) for r in range(rowcount) for g in range(groups) if r >= (near, second)[g]
+    ]
+
     @pl.when(leading)
     def _():
-        auxin[me] = auxout[...]
-        for o in range(1, blocks):
-            b = lax.rem(me + o, blocks)
+        def arrived(b, source, target, send, recv):
             pltpu.make_async_remote_copy(
-                src_ref=auxout, dst_ref=auxin.at[b],
-                send_sem=aux_send.at[0], recv_sem=aux_recv.at[b],
+                src_ref=source, dst_ref=target.at[b], send_sem=send.at[0], recv_sem=recv.at[b],
                 device_id=block(b), device_id_type=MESH,
             ).wait_recv()
 
+        def await_rows(part, source, target, send, recv):
+            if part == 0:
+                for k in range(leaders - 1):
+                    arrived(place_of(another(k)), source, target, send, recv)
+            for g, r in outside:
+                if r * 2 // rowcount == part:
+                    arrived(g * rowcount + r, source, target, send, recv)
+
         own = tile_iota(1) % SUB == tile_iota(0)
-        for k in range(2):
-            high, middle, _ = thirds(auxin[:, k, :])
-            wide[0, k * blocks : (k + 1) * blocks] = high
-            wide[1, k * blocks : (k + 1) * blocks] = middle
-        pieces = [
-            jnp.concatenate(
-                [jnp.where(own, wide[part, k : k + 1, :], 0.0) for k in range(2 * blocks)], axis=0
+        half = rowcount // 2
+
+        def expand(part):
+            rows = [(k, p * rowcount + part * half) for k in range(2) for p in range(groups)]
+            for at, (k, begin) in enumerate(rows):
+                high, middle, _ = thirds(auxin[begin : begin + half, k, :])
+                wide[0, at * half : (at + 1) * half] = high
+                wide[1, at * half : (at + 1) * half] = middle
+            pieces = [
+                jnp.concatenate(
+                    [
+                        jnp.where(own, wide[which, k : k + 1, :], 0.0)
+                        for k in range(len(rows) * half)
+                    ],
+                    axis=0,
+                )
+                for which in range(2)
+            ]
+            tiles = jnp.dot(
+                jnp.concatenate(pieces, axis=1), spread[...], preferred_element_type=jnp.float32
             )
-            for part in range(2)
-        ]
-        tiles = jnp.dot(
-            jnp.concatenate(pieces, axis=1), spread[...], preferred_element_type=jnp.float32
-        )
-        tiles = [tiles[k * SUB : (k + 1) * SUB] for k in range(2 * blocks)]
-        for q in range(rowcount):
-            for k, m in enumerate(paired(tiles[q], tiles[rowcount + q])):
-                y = CY * q + k
-                m_z = turned(m, SUB)
-                low, low_z = turned(m, 1, 0), turned(m_z, 1, 0)
-                masses[y], masses_z[y] = m, m_z
-                lows[y], lows_z[y] = low, low_z
-                boths[y], boths_z[y] = m + low, m_z + low_z
-        for q in range(rowcount):
-            reacts = paired(tiles[blocks + q], tiles[blocks + rowcount + q])
-            for k, react in enumerate(reacts):
-                y = CY * q + k
-                around = (boths[y] + boths_z[y]) + (boths[(y - 1) % planes] + boths_z[(y - 1) % planes])
-                diag[y] = react - 4.0 * around
-
-        inbox[me] = outbox[rank]
-        for o in range(1, blocks):
-            b = lax.rem(me + o, blocks)
-            pltpu.make_async_remote_copy(
-                src_ref=outbox.at[0], dst_ref=inbox.at[b],
-                send_sem=out_send.at[0], recv_sem=out_recv.at[b],
-                device_id=block(b), device_id_type=MESH,
-            ).wait_recv()
-        for q in range(rowcount):
-            for k, value in enumerate(paired(inbox[q], inbox[rowcount + q])):
-                bases[0, CY * q + k] = value
-
-        def apply_operator(source, sink):
-            taken = {}
+            tiles = [tiles[k * SUB : (k + 1) * SUB] for k in range(len(rows) * half)]
+            for q in range(half):
+                for k, m in enumerate(paired(tiles[q], tiles[half + q])):
+                    y = CY * (part * half + q) + k
+                    m_z = turned(m, SUB)
+                    low, low_z = turned(m, 1, 0), turned(m_z, 1, 0)
+                    masses[y], masses_z[y] = m, m_z
+                    lows[y], lows_z[y] = low, low_z
+                    boths[y], boths_z[y] = m + low, m_z + low_z
+                for k, react in enumerate(paired(tiles[2 * half + q], tiles[3 * half + q])):
+                    diag[CY * (part * half + q) + k] = react
+
+        def settle(ys):
+            for y in ys:
+                z = (y - 1) % planes
+                diag[y] = diag[y] - 4.0 * ((boths[y] + boths_z[y]) + (boths[z] + boths_z[z]))
+
+        def take_in(part):
+            for q in range(part * half, (part + 1) * half):
+                for k, value in enumerate(paired(inbox[q], inbox[rowcount + q])):
+                    bases[0, CY * q + k] = value
+
+        def apply_operator(source, sink, ys=None, taken=None):
+            taken = {} if taken is None else taken
 
             def around(y):
                 y = y % planes
@@ -378,7 +405,7 @@
                     taken[y] = (v, above, below, v + above, v + below)
                 return taken[y]
 
-            for y in range(planes):
+            for y in range(planes) if ys is None else ys:
                 v, above, below, _, _ = around(y)
                 _, next_above, next_below, next_up, next_down = around(y + 1)
                 _, last_above, last_below, last_up, last_down = around(y - 1)
@@ -397,75 +424,102 @@
                 middle = weighed(boths, boths_z, diagonal) + diag[y] * v
                 sink(y, middle + (ahead + behind))
 
-        scale, steps = chebyshev_steps()
         square, cross = Total(), Total()
 
         def first_image(y, image):
-            residuals[y] = image
+            powers[0, y] = image
             square.add(image * image)
             cross.add(bases[0, y] * image)
 
-        apply_operator(lambda y: bases[0, y], first_image)
+        taken = {}
+        early = range(1, planes // 2 - 1)
+        late = list(range(planes // 2 - 1, planes)) + [0]
+        for part, ready, ys in ((0, range(1, planes // 2), early), (1, list(range(planes // 2, planes)) + [0], late)):
+            if part == 0:
+                auxin[me] = auxout[...]
+                inbox[me] = outbox[rank]
+            await_rows(part, auxout, auxin, aux_send, aux_recv)
+            expand(part)
+            settle(ready)
+            await_rows(part, outbox.at[0], inbox, out_send, out_recv)
+            take_in(part)
+            apply_operator(lambda y: bases[0, y], first_image, ys, taken)
+        def stored(sweep, k):
+            def sink(y, image):
+                powers[sweep * DEGREE + k, y] = image
+
+            return sink
+
+        def mixed(factors, terms):
+            value = factors[0] * terms[0]
+            for factor, term in zip(factors[1:], terms[1:]):
+                value = value + factor * term
+            return value
+
+        apply_operator(lambda y: powers[0, y], stored(0, 1))
         square, cross = summed(square, cross)
         inverse = cross / square
-        opening = scale * inverse
-
-        omegas, squares = [], []
-        for sweep in range(SWEEPS):
-            along, length, begin = Total(), Total(), Total()
-            for step in range(DEGREE):
-                here, there = directions.at[step % 2], directions.at[(step + 1) % 2]
-
-                def finish(y, image, step=step, here=here, there=there, sweep=sweep):
-                    residual = (bases[sweep, y] if step == 0 else residuals[y]) - image
-                    if step + 1 < DEGREE:
-                        direction = here[y]
-                        keep, gain = steps[step]
-                        following = keep * direction + (gain * inverse) * residual
-                        residuals[y] = residual
-                        there[y] = following
-                        so_far = direction if step == 0 else corrections[sweep, y]
-                        corrections[sweep, y] = so_far + following
-                    else:
-                        start = bases[sweep, y]
-                        change = start - residual
-                        changes[y] = change
-                        along.add(start * change)
-                        length.add(change * change)
-
-                if sweep == 0 and step == 0:
-                    for y in range(planes):
-                        here[y] = opening * bases[0, y]
-                        finish(y, opening * residuals[y])
-                else:
-                    apply_operator(lambda y, here=here: here[y], finish)
-            along, length = summed(along, length)
-            omega = along / length
-            omegas.append(omega)
-            if sweep + 1 < SWEEPS:
-                for y in range(planes):
-                    base = bases[sweep, y] - omega * changes[y]
-                    bases[sweep + 1, y] = base
-                    directions[0, y] = opening * base
-                    begin.add(base * base)
-                began = over_z(begin.folded())
+        scales = [inverse]
+        for _ in range(DEGREE - 1):
+            scales.append(scales[-1] * inverse)
+        corrects, differs = chebyshev_weights()
+        corrects = [b * scale for b, scale in zip(corrects, scales)]
+        differs = [c * scale for c, scale in zip(differs, scales)]
+
+        def closing(sweep, along, length):
+            def sink(y, image):
+                begin = sweep * DEGREE
+                terms = [powers[begin + k, y] for k in range(DEGREE - 1)]
+                start = bases[sweep, y]
+                change = mixed(differs, terms + [image])
+                along.add(start * change)
+                length.add(change * change)
+                changes[y] = change
+                corrections[sweep, y] = mixed(corrects, [start] + terms)
+
+            return sink
+
+        apply_operator(lambda y: powers[1, y], stored(0, 2))
+        along, length = Total(), Total()
+        apply_operator(lambda y: powers[2, y], closing(0, along, length))
+        apply_operator(lambda y: changes[y], stored(0, 3))
+        along, length = summed(along, length)
+        omega = along / length
+        begin = Total()
+
+        def second_start(y):
+            base = bases[0, y] - omega * changes[y]
+            bases[1, y] = base
+            begin.add(base * base)
+            image = powers[0, y] - omega * powers[3, y]
+            powers[DEGREE, y] = image
+            return image
+
+        apply_operator(second_start, stored(1, 1))
+        began = over_z(begin.folded())
+        apply_operator(lambda y: powers[DEGREE + 1, y], stored(1, 2))
+        along, length = Total(), Total()
+        apply_operator(lambda y: powers[DEGREE + 2, y], closing(1, along, length))
+        for q in range(rowcount):
+            for sweep in range(SWEEPS):
+                halves = [corrections[sweep, CY * q + k] for k in range(CY)]
+                if sweep == 0:
+                    halves = [omega * value for value in halves]
+                for p, tile in enumerate(paired(*halves)):
+                    mixes[sweep, p * rowcount + q] = tile
+        along, length = summed(along, length)
+        omega = along / length
         group = tile_iota(1) // SUB
         last = jnp.maximum(began - omega * along, 0.0)
         rms = jnp.where(group == rank, began, jnp.where(group == rank + leaders, last, 0.0))
         rms = jnp.sqrt(rms / total)[0:1]
-        for q in range(rowcount):
-            values = [
-                omegas[0] * corrections[0, CY * q + k] + omegas[1] * corrections[1, CY * q + k]
-                for k in range(CY)
-            ]
-            for p, tile in enumerate(paired(*values)):
-                solved[p * rowcount + q, 0:SUB] = tile
-                solved[p * rowcount + q, SUB : SUB + 1] = rms
-        for o in range(1, leaders):
-            reply(place_of(lax.rem(rank + o, leaders))).start()
-        for g in range(groups):
-            for r in range(heads, rowcount):
-                reply(g * rowcount + r).start()
+        for b in range(blocks):
+            solved[b, 0:SUB] = mixes[0, b] + omega * mixes[1, b]
+            solved[b, SUB : SUB + 1] = rms
+        for k in range(leaders - 1):
+            reply(place_of(another(k))).start()
+        for g, r in outside:
+            reply(g * rowcount + r).start()
         answers[rank] = solved[me]
 
     def await_reply(t):
@@ -475,12 +529,15 @@
             device_id=leader(t), device_id_type=MESH,
         ).wait_recv()
 
-    for o in range(1, leaders):
-        await_reply(lax.rem(rank + o, leaders))
+    @pl.when(leading)
+    def _():
+        for k in range(leaders - 1):
+            await_reply(another(k))
 
     @pl.when(jnp.logical_not(leading))
     def _():
-        await_reply(lax.rem(rank, leaders))
+        for t in range(leaders):
+            await_reply(t)
 
     whole = jnp.concatenate([exchanged(answers[t, 0:SUB]) for t in range(leaders)], axis=0)
     whole = jnp.concatenate(thirds(whole), axis=0)
@@ -494,13 +551,7 @@
     other = turned(line, count // 2)
     rms_ref[...] = jnp.concatenate([line, other], axis=0)[:, :nrhs]
 
-    for send in (post_aux, post_field):
-        for o in range(1, leaders):
-            send(o).wait_send()
-
-        @pl.when(jnp.logical_not(leading))
-        def _(send=send):
-            send(0).wait_send()
+    each_post(lambda copy: copy.wait_send())
 
     @pl.when(leading)
     def _():
@@ -544,7 +595,8 @@
             space(leaders, SUB + 1, count), space(blocks, SUB + 1, count),
             space(count, count), space(2 * count, count), space(2, 2 * blocks, count),
             plane, plane, plane, plane, plane, plane, plane,
-            twice, plane, space(2, planes, SUB, count), twice, plane,
+            twice, plane, twice, space(SWEEPS * DEGREE, planes, SUB, count),
+            space(SWEEPS, blocks, SUB, count),
             dma((4,)), dma((leaders,)), dma((blocks,)), dma((leaders,)), dma((blocks,)),
             dma((blocks,)), dma((leaders,)),
         ],

time: 18.1 us -> 17 us (0.939)
  Pallas kernels: 17.2 us -> 16.2 us
    pallas_call x1, Pallas kernels: 16.6 us -> 15.5 us  [whole_sweeps(): pl.pallas_call(functools.partial(kernel, groups, rowcount, count * groups...]
where the time goes in v4:
time: 17 us; the launch traced here: 16.8 us
  Pallas kernels  16.2 us (95%)
  between operations  0.64 us (4%)
    pallas_call x1, Pallas kernels, whole_sweeps(): pl.pallas_call(functools.partial(kernel, groups, rowcount, count * groups...  15.5 us
    pallas_call x1, Pallas kernels, whole_sweeps(): pl.pallas_call(write_out, out_shape=(jax.ShapeDtypeStruct((nrhs, count),...  0.64 us

profile of v4, /device:TPU:0, one launch (start us, length us, event | category | flops | bytes accessed | tf_op | source)
XLA Modules:
  0.0 16.8 jit_solution(13255619186303468636)
XLA Ops:
  0.6 15.5 %shard_map.59 = (f32[64,128]{1,0:T(8,128)S(1)}, f32[2,64]{1,0:T(2,128)S(1)}) custom-call(f32[64,128]{1,0:T(8,128)} %right_hbm.1, s32[8,128]{1,0:T(8,128)} %links_hbm.1, f32[1,128]{1,0:T(1,128)} %bitcast.2, f32[1,128]{1,0:T(1,128)} %bitcast.3), custom_call_target="tpu_custom_call" | custom-call | tf_op jit(solution)/shard_map/pallas_call | solution.py:586
  16.2 0.6 %shard_map.60 = (f32[64,128]{1,0:T(8,128)}, f32[2,64]{1,0:T(2,128)}) custom-call(f32[64,128]{1,0:T(8,128)S(1)} %get-tuple-element.4.solution_ref, f32[2,64]{1,0:T(2,128)S(1)} %get-tuple-element.5.rms_ref), custom_call_target="tpu_custom_call" | custom-call | tf_op jit(solution)/shard_map/pallas_call | solution.py:605

commit v5 on v4

--- a/solution.py
+++ b/solution.py
@@ -292,41 +292,53 @@
     auxout[...] = jnp.concatenate([mass, react], axis=0)
     field = added([stack[SUB + k * nrhs : SUB + (k + 1) * nrhs] for k in range(3)])
 
+    own_part = jnp.where(row < rowcount // 2, 0, 1)
+
     def post(t, source, target, send, recv):
         return pltpu.make_async_remote_copy(
-            src_ref=source(t), dst_ref=target.at[me], send_sem=send.at[t], recv_sem=recv,
+            src_ref=source(t), dst_ref=target.at[me], send_sem=send, recv_sem=recv,
             device_id=leader(t), device_id_type=MESH,
         )
 
     def post_aux(t):
-        return post(t, lambda t: auxout, auxin, aux_send, aux_recv.at[me])
+        return post(t, lambda t: auxout, auxin, aux_send, aux_recv.at[own_part])
 
     def post_field(t):
-        return post(t, lambda t: outbox.at[t], inbox, out_send, out_recv.at[me])
-
-    def each_post(act):
+        return post(t, lambda t: outbox.at[t], inbox, out_send, out_recv.at[own_part])
+
+    def start_posts():
         for send in (post_aux, post_field):
 
             @pl.when(leading)
             def _(send=send):
                 for k in range(leaders - 1):
-                    act(send(another(k)))
+                    send(another(k)).start()
 
             @pl.when(jnp.logical_not(leading))
             def _(send=send):
                 for t in range(leaders):
-                    act(send(t))
+                    send(t).start()
+
+    def whole_of(ref, number, send, recv):
+        return pltpu.make_async_remote_copy(
+            src_ref=ref.at[pl.ds(0, number)], dst_ref=ref.at[pl.ds(0, number)],
+            send_sem=send, recv_sem=recv, device_id=leader(0), device_id_type=MESH,
+        )
+
+    def sent_posts(number):
+        whole_of(auxin, number, aux_send, aux_recv.at[0]).wait_send()
+        whole_of(inbox, number, out_send, out_recv.at[0]).wait_send()
 
     for t in range(leaders):
         outbox[t] = exchanged(field[t * SUB : (t + 1) * SUB])
     pl.semaphore_wait(barrier, jnp.where(leading, leaders - 1, leaders))
 
-    each_post(lambda copy: copy.start())
+    start_posts()
 
     def reply(b):
         return pltpu.make_async_remote_copy(
             src_ref=solved.at[b], dst_ref=answers.at[rank],
-            send_sem=back_send.at[b], recv_sem=back_recv.at[rank],
+            send_sem=back_send, recv_sem=back_recv,
             device_id=block(b), device_id_type=MESH,
         )
 
@@ -336,19 +348,8 @@
 
     @pl.when(leading)
     def _():
-        def arrived(b, source, target, send, recv):
-            pltpu.make_async_remote_copy(
-                src_ref=source, dst_ref=target.at[b], send_sem=send.at[0], recv_sem=recv.at[b],
-                device_id=block(b), device_id_type=MESH,
-            ).wait_recv()
-
-        def await_rows(part, source, target, send, recv):
-            if part == 0:
-                for k in range(leaders - 1):
-                    arrived(place_of(another(k)), source, target, send, recv)
-            for g, r in outside:
-                if r * 2 // rowcount == part:
-                    arrived(g * rowcount + r, source, target, send, recv)
+        def await_rows(part, target, send, recv):
+            whole_of(target, blocks // 2 - 1 + part, send, recv.at[part]).wait_recv()
 
         own = tile_iota(1) % SUB == tile_iota(0)
         half = rowcount // 2
@@ -438,10 +439,10 @@
             if part == 0:
                 auxin[me] = auxout[...]
                 inbox[me] = outbox[rank]
-            await_rows(part, auxout, auxin, aux_send, aux_recv)
+            await_rows(part, auxin, aux_send, aux_recv)
             expand(part)
             settle(ready)
-            await_rows(part, outbox.at[0], inbox, out_send, out_recv)
+            await_rows(part, inbox, out_send, out_recv)
             take_in(part)
             apply_operator(lambda y: bases[0, y], first_image, ys, taken)
         def stored(sweep, k):
@@ -522,22 +523,16 @@
             reply(g * rowcount + r).start()
         answers[rank] = solved[me]
 
-    def await_reply(t):
-        pltpu.make_async_remote_copy(
-            src_ref=solved.at[0], dst_ref=answers.at[t],
-            send_sem=back_send.at[0], recv_sem=back_recv.at[t],
-            device_id=leader(t), device_id_type=MESH,
-        ).wait_recv()
+    def answered(number):
+        whole_of(answers, number, back_send, back_recv).wait_recv()
 
     @pl.when(leading)
     def _():
-        for k in range(leaders - 1):
-            await_reply(another(k))
+        answered(leaders - 1)
 
     @pl.when(jnp.logical_not(leading))
     def _():
-        for t in range(leaders):
-            await_reply(t)
+        answered(leaders)
 
     whole = jnp.concatenate([exchanged(answers[t, 0:SUB]) for t in range(leaders)], axis=0)
     whole = jnp.concatenate(thirds(whole), axis=0)
@@ -551,12 +546,14 @@
     other = turned(line, count // 2)
     rms_ref[...] = jnp.concatenate([line, other], axis=0)[:, :nrhs]
 
-    each_post(lambda copy: copy.wait_send())
-
     @pl.when(leading)
     def _():
-        for o in range(1, blocks):
-            reply(lax.rem(me + o, blocks)).wait_send()
+        sent_posts(leaders - 1)
+        whole_of(solved, blocks - 1, back_send, back_recv).wait_send()
+
+    @pl.when(jnp.logical_not(leading))
+    def _():
+        sent_posts(leaders)
 
 
 def write_out(solution_ref, rms_ref, out_hbm, rms_hbm, sems):
@@ -597,8 +594,7 @@
             plane, plane, plane, plane, plane, plane, plane,
             twice, plane, twice, space(SWEEPS * DEGREE, planes, SUB, count),
             space(SWEEPS, blocks, SUB, count),
-            dma((4,)), dma((leaders,)), dma((blocks,)), dma((leaders,)), dma((blocks,)),
-            dma((blocks,)), dma((leaders,)),
+            dma((4,)), dma, dma((2,)), dma, dma((2,)), dma, dma,
         ],
         compiler_params=pltpu.CompilerParams(collective_id=0, has_side_effects=True),
     )(right_side, links, coefs.reshape(1, count), reaction.reshape(1, count))

time: 17 us -> 16 us (0.941)
  Pallas kernels: 16.2 us -> 15.2 us
    pallas_call x1, Pallas kernels: 15.5 us -> 14.5 us  [whole_sweeps(): pl.pallas_call(functools.partial(kernel, groups, rowcount, count * groups...]
where the time goes in v5:
time: 16 us; the launch traced here: 15.8 us
  Pallas kernels  15.2 us (95%)
  between operations  0.64 us (4%)
    pallas_call x1, Pallas kernels, whole_sweeps(): pl.pallas_call(functools.partial(kernel, groups, rowcount, count * groups...  14.5 us
    pallas_call x1, Pallas kernels, whole_sweeps(): pl.pallas_call(write_out, out_shape=(jax.ShapeDtypeStruct((nrhs, count),...  0.64 us

profile of v5, /device:TPU:0, one launch (start us, length us, event | category | flops | bytes accessed | tf_op | source)
XLA Modules:
  0.0 15.8 jit_solution(4978656652279249669)
XLA Ops:
  0.6 14.5 %shard_map.59 = (f32[64,128]{1,0:T(8,128)S(1)}, f32[2,64]{1,0:T(2,128)S(1)}) custom-call(f32[64,128]{1,0:T(8,128)} %right_hbm.1, s32[8,128]{1,0:T(8,128)} %links_hbm.1, f32[1,128]{1,0:T(1,128)} %bitcast.2, f32[1,128]{1,0:T(1,128)} %bitcast.3), custom_call_target="tpu_custom_call" | custom-call | tf_op jit(solution)/shard_map/pallas_call | solution.py:583
  15.2 0.6 %shard_map.60 = (f32[64,128]{1,0:T(8,128)}, f32[2,64]{1,0:T(2,128)}) custom-call(f32[64,128]{1,0:T(8,128)S(1)} %get-tuple-element.4.solution_ref, f32[2,64]{1,0:T(2,128)S(1)} %get-tuple-element.5.rms_ref), custom_call_target="tpu_custom_call" | custom-call | tf_op jit(solution)/shard_map/pallas_call | solution.py:601

commit v6 on v5

--- a/solution.py
+++ b/solution.py
@@ -162,7 +162,7 @@
     )
 
 
-def chebyshev_weights():
+def correction_weights():
     center, half = (1.5 + 0.15) / 2.0, (1.5 - 0.15) / 2.0
     sigma = center / half
     rho_now = 1.0 / sigma
@@ -175,7 +175,7 @@
         rho_next = 1.0 / (2.0 * sigma - rho_now)
         direction = rho_next * rho_now * direction + 2.0 * rho_next / half * residual
         rho_now = rho_next
-    return [float(b) for b in correction[:DEGREE]], [-float(c) for c in residual[1:]]
+    return [float(b / correction[DEGREE - 1]) for b in correction[: DEGREE - 1]]
 
 
 class Total:
@@ -216,7 +216,7 @@
     solution_ref, rms_ref,
     right_ref, links_ref, coefs_ref, react_ref,
     auxout, auxin, outbox, inbox, answers, solved, order, spread, wide,
-    masses, masses_z, lows, lows_z, boths, boths_z, diag,
+    masses, masses_z, flats, flats_z, talls, edges_x, edges_y, edges_z, edges_below, diag,
     bases, changes, corrections, powers, mixes,
     in_sem, aux_send, aux_recv, out_send, out_recv, back_send, back_recv,
 ):
@@ -282,7 +282,7 @@
         load.wait()
     slots = to_lanes(links_ref[0:1, :] - me * count)
     order[...] = (down == slots).astype(jnp.float32)
-    mass = to_lanes(coefs_ref[...] * (-1.0 / 12.0))
+    mass = to_lanes(coefs_ref[...] * (1.0 / 12.0))
     react = thirds(react_ref[...])
     react = jnp.concatenate(react + [jnp.zeros((SUB - 3, count), jnp.float32)], axis=0)
     loads[3].wait()
@@ -378,73 +378,64 @@
                 for k, m in enumerate(paired(tiles[q], tiles[half + q])):
                     y = CY * (part * half + q) + k
                     m_z = turned(m, SUB)
-                    low, low_z = turned(m, 1, 0), turned(m_z, 1, 0)
+                    flat, flat_z = m + turned(m, 1, 0), m_z + turned(m_z, 1, 0)
                     masses[y], masses_z[y] = m, m_z
-                    lows[y], lows_z[y] = low, low_z
-                    boths[y], boths_z[y] = m + low, m_z + low_z
+                    flats[y], flats_z[y] = flat, flat_z
+                    talls[y], edges_y[y] = m + m_z, flat + flat_z
                 for k, react in enumerate(paired(tiles[2 * half + q], tiles[3 * half + q])):
                     diag[CY * (part * half + q) + k] = react
 
         def settle(ys):
             for y in ys:
                 z = (y - 1) % planes
-                diag[y] = diag[y] - 4.0 * ((boths[y] + boths_z[y]) + (boths[z] + boths_z[z]))
+                edges_x[y] = talls[y] + talls[z]
+                edges_z[y] = flats[y] + flats[z]
+                edges_below[y] = flats_z[y] + flats_z[z]
+                diag[y] = diag[y] + 5.0 * (edges_y[y] + edges_y[z])
 
         def take_in(part):
             for q in range(part * half, (part + 1) * half):
                 for k, value in enumerate(paired(inbox[q], inbox[rowcount + q])):
                     bases[0, CY * q + k] = value
 
-        def apply_operator(source, sink, ys=None, taken=None):
-            taken = {} if taken is None else taken
+        def apply_operator(source, sink, ys):
+            taken, pushed = {}, {}
 
             def around(y):
                 y = y % planes
                 if y not in taken:
                     v = source(y)
                     above, below = turned(v, -SUB), turned(v, SUB)
-                    taken[y] = (v, above, below, v + above, v + below)
+                    up, down = v + above, v + below
+                    up, down = up + turned(up, -1, 0), down + turned(down, -1, 0)
+                    taken[y] = (v, above, below, up, down)
                 return taken[y]
 
-            for y in range(planes) if ys is None else ys:
+            def push(y):
+                y = y % planes
+                if y not in pushed:
+                    (_, _, _, up, down), (_, _, _, next_up, next_down) = around(y), around(y + 1)
+                    pushed[y] = masses[y] * (up + next_up) + masses_z[y] * (down + next_down)
+                return pushed[y]
+
+            for y in ys:
                 v, above, below, _, _ = around(y)
-                _, next_above, next_below, next_up, next_down = around(y + 1)
-                _, last_above, last_below, last_up, last_down = around(y - 1)
-                sides = [above + next_up, below + next_down, above + last_up, below + last_down]
-                diagonal = [next_above, next_below, last_above, last_below]
-
-                def weighed(a, b, values, y=y):
-                    z = (y - 1) % planes
-                    products = [
-                        c * value for c, value in zip((a[y], b[y], a[z], b[z]), values)
-                    ]
-                    return (products[0] + products[1]) + (products[2] + products[3])
-
-                ahead = turned(weighed(lows, lows_z, sides), -1, 0)
-                behind = turned(weighed(masses, masses_z, sides), 1, 0)
-                middle = weighed(boths, boths_z, diagonal) + diag[y] * v
-                sink(y, middle + (ahead + behind))
+                both = push(y) + push(y - 1)
+                edge_x = edges_x[y]
+                image = (diag[y] * v + edges_z[y] * above) + edges_below[y] * below
+                image = image + (
+                    edges_y[y] * around(y + 1)[0] + edges_y[(y - 1) % planes] * around(y - 1)[0]
+                )
+                image = image + (edge_x * turned(v, -1, 0) - both)
+                sink(y, image + turned(edge_x * v - both, 1, 0))
 
         square, cross = Total(), Total()
 
-        def first_image(y, image):
+        def opening_image(y, image):
             powers[0, y] = image
             square.add(image * image)
             cross.add(bases[0, y] * image)
 
-        taken = {}
-        early = range(1, planes // 2 - 1)
-        late = list(range(planes // 2 - 1, planes)) + [0]
-        for part, ready, ys in ((0, range(1, planes // 2), early), (1, list(range(planes // 2, planes)) + [0], late)):
-            if part == 0:
-                auxin[me] = auxout[...]
-                inbox[me] = outbox[rank]
-            await_rows(part, auxin, aux_send, aux_recv)
-            expand(part)
-            settle(ready)
-            await_rows(part, inbox, out_send, out_recv)
-            take_in(part)
-            apply_operator(lambda y: bases[0, y], first_image, ys, taken)
         def stored(sweep, k):
             def sink(y, image):
                 powers[sweep * DEGREE + k, y] = image
@@ -457,33 +448,65 @@
                 value = value + factor * term
             return value
 
-        apply_operator(lambda y: powers[0, y], stored(0, 1))
+        def ring(begin):
+            return [(begin + k) % planes for k in range(planes)]
+
+        def early(k):
+            return range(k, planes // 2 - k)
+
+        def late(k):
+            return [y for y in ring(planes // 2 - k) if y not in early(k)]
+
+        def start_plane(y):
+            return bases[0, y]
+
+        def first_image(y):
+            return powers[0, y]
+
+        auxin[me] = auxout[...]
+        inbox[me] = outbox[rank]
+        for part, ys in ((0, range(1, planes // 2)), (1, ring(planes // 2)[: planes // 2 + 1])):
+            await_rows(part, auxin, aux_send, aux_recv)
+            expand(part)
+            settle(ys)
+            await_rows(part, inbox, out_send, out_recv)
+            take_in(part)
+            if part == 0:
+                apply_operator(start_plane, opening_image, early(1))
+                apply_operator(first_image, stored(0, 1), early(2))
+                apply_operator(lambda y: powers[1, y], stored(0, 2), early(3))
+        apply_operator(start_plane, opening_image, late(1))
         square, cross = summed(square, cross)
-        inverse = cross / square
-        scales = [inverse]
-        for _ in range(DEGREE - 1):
-            scales.append(scales[-1] * inverse)
-        corrects, differs = chebyshev_weights()
-        corrects = [b * scale for b, scale in zip(corrects, scales)]
-        differs = [c * scale for c, scale in zip(differs, scales)]
-
-        def closing(sweep, along, length):
-            def sink(y, image):
+        theta = square / cross
+        scales = [theta]
+        for _ in range(DEGREE - 2):
+            scales.append(scales[-1] * theta)
+        factors = [b * scale for b, scale in zip(correction_weights(), scales[::-1])]
+
+        def corrected(sweep):
+            def source(y):
                 begin = sweep * DEGREE
-                terms = [powers[begin + k, y] for k in range(DEGREE - 1)]
-                start = bases[sweep, y]
-                change = mixed(differs, terms + [image])
-                along.add(start * change)
+                terms = [bases[sweep, y]] + [powers[begin + k, y] for k in range(DEGREE - 2)]
+                value = powers[begin + DEGREE - 2, y] + mixed(factors, terms)
+                corrections[sweep, y] = value
+                return value
+
+            return source
+
+        def finishing(sweep, along, length):
+            def sink(y, change):
+                along.add(bases[sweep, y] * change)
                 length.add(change * change)
                 changes[y] = change
-                corrections[sweep, y] = mixed(corrects, [start] + terms)
 
             return sink
 
-        apply_operator(lambda y: powers[1, y], stored(0, 2))
         along, length = Total(), Total()
-        apply_operator(lambda y: powers[2, y], closing(0, along, length))
-        apply_operator(lambda y: changes[y], stored(0, 3))
+        apply_operator(first_image, stored(0, 1), late(2))
+        apply_operator(lambda y: powers[1, y], stored(0, 2), late(3))
+        begin_at = planes // 2 - DEGREE + 1
+        apply_operator(corrected(0), finishing(0, along, length), ring(begin_at))
+        apply_operator(lambda y: changes[y], stored(0, 3), ring(begin_at + 1))
         along, length = summed(along, length)
         omega = along / length
         begin = Total()
@@ -496,11 +519,11 @@
             powers[DEGREE, y] = image
             return image
 
-        apply_operator(second_start, stored(1, 1))
+        apply_operator(second_start, stored(1, 1), ring(begin_at + 2))
         began = over_z(begin.folded())
-        apply_operator(lambda y: powers[DEGREE + 1, y], stored(1, 2))
+        apply_operator(lambda y: powers[DEGREE + 1, y], stored(1, 2), ring(begin_at + 3))
         along, length = Total(), Total()
-        apply_operator(lambda y: powers[DEGREE + 2, y], closing(1, along, length))
+        apply_operator(corrected(1), finishing(1, along, length), ring(begin_at + 4))
         for q in range(rowcount):
             for sweep in range(SWEEPS):
                 halves = [corrections[sweep, CY * q + k] for k in range(CY)]
@@ -591,7 +614,7 @@
             space(leaders, SUB, count), space(blocks, SUB, count),
             space(leaders, SUB + 1, count), space(blocks, SUB + 1, count),
             space(count, count), space(2 * count, count), space(2, 2 * blocks, count),
-            plane, plane, plane, plane, plane, plane, plane,
+            plane, plane, plane, plane, plane, plane, plane, plane, plane, plane,
             twice, plane, twice, space(SWEEPS * DEGREE, planes, SUB, count),
             space(SWEEPS, blocks, SUB, count),
             dma((4,)), dma, dma((2,)), dma, dma((2,)), dma, dma,

time: 16 us -> 15.7 us (0.981)
  Pallas kernels: 15.2 us -> 14.8 us
    pallas_call x1, Pallas kernels: 14.5 us -> 14.2 us  [whole_sweeps(): pl.pallas_call(functools.partial(kernel, groups, rowcount, count * groups...]
where the time goes in v6:
time: 15.7 us; the launch traced here: 15.5 us
  Pallas kernels  14.8 us (94%)
  between operations  0.64 us (4%)
    pallas_call x1, Pallas kernels, whole_sweeps(): pl.pallas_call(functools.partial(kernel, groups, rowcount, count * groups...  14.2 us
    pallas_call x1, Pallas kernels, whole_sweeps(): pl.pallas_call(write_out, out_shape=(jax.ShapeDtypeStruct((nrhs, count),...  0.64 us

profile of v6, /device:TPU:0, one launch (start us, length us, event | category | flops | bytes accessed | tf_op | source)
XLA Modules:
  0.0 15.5 jit_solution(14979235042762712751)
XLA Ops:
  0.6 14.2 %shard_map.59 = (f32[64,128]{1,0:T(8,128)S(1)}, f32[2,64]{1,0:T(2,128)S(1)}) custom-call(f32[64,128]{1,0:T(8,128)} %right_hbm.1, s32[8,128]{1,0:T(8,128)} %links_hbm.1, f32[1,128]{1,0:T(1,128)} %bitcast.2, f32[1,128]{1,0:T(1,128)} %bitcast.3), custom_call_target="tpu_custom_call" | custom-call | tf_op jit(solution)/shard_map/pallas_call | solution.py:606
  14.8 0.6 %shard_map.60 = (f32[64,128]{1,0:T(8,128)}, f32[2,64]{1,0:T(2,128)}) custom-call(f32[64,128]{1,0:T(8,128)S(1)} %get-tuple-element.4.solution_ref, f32[2,64]{1,0:T(2,128)S(1)} %get-tuple-element.5.rms_ref), custom_call_target="tpu_custom_call" | custom-call | tf_op jit(solution)/shard_map/pallas_call | solution.py:624

commit v7 on v6

--- a/solution.py
+++ b/solution.py
@@ -218,7 +218,7 @@
     auxout, auxin, outbox, inbox, answers, solved, order, spread, wide,
     masses, masses_z, flats, flats_z, talls, edges_x, edges_y, edges_z, edges_below, diag,
     bases, changes, corrections, powers, mixes,
-    in_sem, aux_send, aux_recv, out_send, out_recv, back_send, back_recv,
+    in_sem, out_send, aux_recv, out_recv, back_send, back_recv,
 ):
     nrhs, count = right_ref.shape
     leaders = nrhs // SUB
@@ -259,8 +259,8 @@
             pl.semaphore_signal(barrier, inc=1, device_id=peer, device_id_type=MESH)
 
     loads = [
-        pltpu.make_async_copy(source, target, in_sem.at[k])
-        for k, (source, target) in enumerate(
+        pltpu.make_async_copy(source, target, in_sem)
+        for source, target in (
             [(links_hbm, links_ref), (coefs_hbm, coefs_ref), (react_hbm, react_ref), (right_hbm, right_ref)]
         )
     ]
@@ -278,14 +278,13 @@
     def to_lanes(line):
         return jnp.take_along_axis(jnp.broadcast_to(line, (SUB, count)), element, axis=1)[0:1]
 
-    for load in loads[:3]:
-        load.wait()
+    everything = spread.at[pl.ds(0, links_ref.shape[0] + 2 + nrhs)]
+    pltpu.make_async_copy(everything, everything, in_sem).wait()
     slots = to_lanes(links_ref[0:1, :] - me * count)
     order[...] = (down == slots).astype(jnp.float32)
     mass = to_lanes(coefs_ref[...] * (1.0 / 12.0))
     react = thirds(react_ref[...])
     react = jnp.concatenate(react + [jnp.zeros((SUB - 3, count), jnp.float32)], axis=0)
-    loads[3].wait()
     stack = jnp.concatenate([react] + thirds(right_ref[...]), axis=0)
     stack = jnp.dot(stack, order[...], preferred_element_type=jnp.float32)
     react = added([stack[k : k + 1] for k in range(3)])
@@ -301,7 +300,7 @@
         )
 
     def post_aux(t):
-        return post(t, lambda t: auxout, auxin, aux_send, aux_recv.at[own_part])
+        return post(t, lambda t: auxout, auxin, out_send, aux_recv.at[own_part])
 
     def post_field(t):
         return post(t, lambda t: outbox.at[t], inbox, out_send, out_recv.at[own_part])
@@ -316,7 +315,7 @@
 
             @pl.when(jnp.logical_not(leading))
             def _(send=send):
-                for t in range(leaders):
+                for t in [*range(near - CY, near), *range(near - CY), *range(near, leaders)]:
                     send(t).start()
 
     def whole_of(ref, number, send, recv):
@@ -326,8 +325,7 @@
         )
 
     def sent_posts(number):
-        whole_of(auxin, number, aux_send, aux_recv.at[0]).wait_send()
-        whole_of(inbox, number, out_send, out_recv.at[0]).wait_send()
+        whole_of(spread, number * (SUB + 2), out_send, out_recv.at[0]).wait_send()
 
     for t in range(leaders):
         outbox[t] = exchanged(field[t * SUB : (t + 1) * SUB])
@@ -342,15 +340,13 @@
             device_id=block(b), device_id_type=MESH,
         )
 
+    leader_blocks = [g * rowcount + r for g, r in map(leader, range(leaders))]
     outside = [
         (g, r) for r in range(rowcount) for g in range(groups) if r >= (near, second)[g]
     ]
 
     @pl.when(leading)
     def _():
-        def await_rows(part, target, send, recv):
-            whole_of(target, blocks // 2 - 1 + part, send, recv.at[part]).wait_recv()
-
         own = tile_iota(1) % SUB == tile_iota(0)
         half = rowcount // 2
 
@@ -466,10 +462,11 @@
         auxin[me] = auxout[...]
         inbox[me] = outbox[rank]
         for part, ys in ((0, range(1, planes // 2)), (1, ring(planes // 2)[: planes // 2 + 1])):
-            await_rows(part, auxin, aux_send, aux_recv)
+            number = blocks // 2 - 1 + part
+            whole_of(auxin, number, out_send, aux_recv.at[part]).wait_recv()
             expand(part)
             settle(ys)
-            await_rows(part, inbox, out_send, out_recv)
+            whole_of(inbox, number, out_send, out_recv.at[part]).wait_recv()
             take_in(part)
             if part == 0:
                 apply_operator(start_plane, opening_image, early(1))
@@ -537,13 +534,23 @@
         last = jnp.maximum(began - omega * along, 0.0)
         rms = jnp.where(group == rank, began, jnp.where(group == rank + leaders, last, 0.0))
         rms = jnp.sqrt(rms / total)[0:1]
-        for b in range(blocks):
+
+        def settled(b):
             solved[b, 0:SUB] = mixes[0, b] + omega * mixes[1, b]
             solved[b, SUB : SUB + 1] = rms
-        for k in range(leaders - 1):
-            reply(place_of(another(k))).start()
-        for g, r in outside:
-            reply(g * rowcount + r).start()
+
+        for group in (leader_blocks[:CY], leader_blocks[CY:]):
+            for b in group:
+                settled(b)
+            for b in group:
+
+                @pl.when(me != b)
+                def _(b=b):
+                    reply(b).start()
+
+        for b in [g * rowcount + r for g, r in sorted(outside, key=lambda p: (p[1] % CX, p[1]))]:
+            settled(b)
+            reply(b).start()
         answers[rank] = solved[me]
 
     def answered(number):
@@ -617,7 +624,7 @@
             plane, plane, plane, plane, plane, plane, plane, plane, plane, plane,
             twice, plane, twice, space(SWEEPS * DEGREE, planes, SUB, count),
             space(SWEEPS, blocks, SUB, count),
-            dma((4,)), dma, dma((2,)), dma, dma((2,)), dma, dma,
+            dma, dma, dma((2,)), dma((2,)), dma, dma,
         ],
         compiler_params=pltpu.CompilerParams(collective_id=0, has_side_effects=True),
     )(right_side, links, coefs.reshape(1, count), reaction.reshape(1, count))

time: 15.7 us -> 15.7 us (level)
  no operation moved by 1% of the time
where the time goes in v7:
time: 15.7 us; the launch traced here: 15.5 us
  Pallas kernels  14.9 us (95%)
  between operations  0.64 us (4%)
    pallas_call x1, Pallas kernels, whole_sweeps(): pl.pallas_call(functools.partial(kernel, groups, rowcount, count * groups...  14.2 us
    pallas_call x1, Pallas kernels, whole_sweeps(): pl.pallas_call(write_out, out_shape=(jax.ShapeDtypeStruct((nrhs, count),...  0.64 us

profile of v7, /device:TPU:0, one launch (start us, length us, event | category | flops | bytes accessed | tf_op | source)
XLA Modules:
  0.0 15.5 jit_solution(15153211968870657146)
XLA Ops:
  0.6 14.2 %shard_map.59 = (f32[64,128]{1,0:T(8,128)S(1)}, f32[2,64]{1,0:T(2,128)S(1)}) custom-call(f32[64,128]{1,0:T(8,128)} %right_hbm.1, s32[8,128]{1,0:T(8,128)} %links_hbm.1, f32[1,128]{1,0:T(1,128)} %bitcast.2, f32[1,128]{1,0:T(1,128)} %bitcast.3), custom_call_target="tpu_custom_call" | custom-call | tf_op jit(solution)/shard_map/pallas_call | solution.py:613
  14.9 0.6 %shard_map.60 = (f32[64,128]{1,0:T(8,128)}, f32[2,64]{1,0:T(2,128)}) custom-call(f32[64,128]{1,0:T(8,128)S(1)} %get-tuple-element.4.solution_ref, f32[2,64]{1,0:T(2,128)S(1)} %get-tuple-element.5.rms_ref), custom_call_target="tpu_custom_call" | custom-call | tf_op jit(solution)/shard_map/pallas_call | solution.py:631

commit v8 on v7

--- a/solution.py
+++ b/solution.py
@@ -548,7 +548,7 @@
                 def _(b=b):
                     reply(b).start()
 
-        for b in [g * rowcount + r for g, r in sorted(outside, key=lambda p: (p[1] % CX, p[1]))]:
+        for b in [g * rowcount + r for g, r in sorted(outside, key=lambda p: -(p[0] + p[1] % CX // 2 + min(p[1] // CX, rowcount // CX - p[1] // CX)))]:
             settled(b)
             reply(b).start()
         answers[rank] = solved[me]

time: 15.7 us -> 15.7 us (level)
  no operation moved by 1% of the time
where the time goes in v8:
time: 15.7 us; the launch traced here: 15.5 us
  Pallas kernels  14.9 us (95%)
  between operations  0.64 us (4%)
    pallas_call x1, Pallas kernels, whole_sweeps(): pl.pallas_call(functools.partial(kernel, groups, rowcount, count * groups...  14.2 us
    pallas_call x1, Pallas kernels, whole_sweeps(): pl.pallas_call(write_out, out_shape=(jax.ShapeDtypeStruct((nrhs, count),...  0.64 us

profile of v8, /device:TPU:0, one launch (start us, length us, event | category | flops | bytes accessed | tf_op | source)
XLA Modules:
  0.0 15.5 jit_solution(3816333161368733202)
XLA Ops:
  0.6 14.2 %shard_map.59 = (f32[64,128]{1,0:T(8,128)S(1)}, f32[2,64]{1,0:T(2,128)S(1)}) custom-call(f32[64,128]{1,0:T(8,128)} %right_hbm.1, s32[8,128]{1,0:T(8,128)} %links_hbm.1, f32[1,128]{1,0:T(1,128)} %bitcast.2, f32[1,128]{1,0:T(1,128)} %bitcast.3), custom_call_target="tpu_custom_call" | custom-call | tf_op jit(solution)/shard_map/pallas_call | solution.py:613
  14.9 0.6 %shard_map.60 = (f32[64,128]{1,0:T(8,128)}, f32[2,64]{1,0:T(2,128)}) custom-call(f32[64,128]{1,0:T(8,128)S(1)} %get-tuple-element.4.solution_ref, f32[2,64]{1,0:T(2,128)S(1)} %get-tuple-element.5.rms_ref), custom_call_target="tpu_custom_call" | custom-call | tf_op jit(solution)/shard_map/pallas_call | solution.py:631
